TPU v7x, 32 devices: a whole 2x2x4 slice. The times are simulated.
32 devices in a mesh: gx: 4 (over y, core), gy: 2 (over x), gz: 4 (over z).
Axes of the slice: x: 2, y: 2, z: 4, core: 2. Of those that a mesh axis runs over, the one named last changes fastest.
Arguments:
- noisy_image: float32 [32, 64, 512], P('gz', 'gy', 'gx'), may hold values from -6 to 6
- fidelity: float32 [32, 64, 512], P('gz', 'gy', 'gx'), may hold values from 0.5 to 8
- primal_u: float32 [32, 64, 512], P('gz', 'gy', 'gx'), may hold values from -6 to 6
- primal_v: float32 [3, 32, 64, 512], P(None, 'gz', 'gy', 'gx'), may hold values from -2 to 2
- dual_p: float32 [3, 32, 64, 512], P(None, 'gz', 'gy', 'gx'), may hold values from -2.5 to 2.5
- dual_q: float32 [6, 32, 64, 512], P(None, 'gz', 'gy', 'gx'), may hold values from -2.5 to 2.5
Outputs:
- denoised: float32 [32, 64, 512], P('gz', 'gy', 'gx')
- vector_field: float32 [3, 32, 64, 512], P(None, 'gz', 'gy', 'gx')
- grad_dual: float32 [3, 32, 64, 512], P(None, 'gz', 'gy', 'gx')
- sym_dual: float32 [6, 32, 64, 512], P(None, 'gz', 'gy', 'gx')
All inputs are finite; a program needn't handle non-finite values.
Results may differ from a plain program's by a relative error of at most 0.0001.
Values sent between devices are 32-bit elements; how exact they have to be, the bound alone decides.
A program may use at most 64 MiB of HBM per device.

v0:
```python
import functools

import jax
import jax.numpy as jnp
from jax import lax
from jax.experimental import pallas as pl
from jax.experimental.pallas import tpu as pltpu
from jax.sharding import PartitionSpec as P

ITERS = 3
AXES = ("gx", "gy", "gz")
ALPHA1, ALPHA0, SIGMA, TAU = 0.5, 1.0, 0.2, 0.2
Q_FROM = (0, 3, 1, 5, 2, 4)
GROUP = 4
XX, XY, YY, YZ, ZZ, XZ = range(6)
MESH = pl.DeviceIdType.MESH
TOP = 8


def kernel(
    noisy_in, fid_in, u_in, v_in, p_in, q_in,
    u_out, v_out, p_out, q_out,
    bar, pp, qq, gain, offset, partial,
    send_u, send_v, send_p, send_q, got_u, got_v, got_p, got_q,
    load_sem, send_sem, recv_sem,
):
    zs, ys, xs = u_in.shape
    blocks = ys // 8
    place = [lax.axis_index(a) for a in AXES]
    count = [lax.axis_size(a) for a in AXES]
    below = [place[i] > 0 for i in range(3)]
    above = [place[i] < count[i] - 1 for i in range(3)]

    peers = sum(there.astype(jnp.int32) for there in below + above)

    barrier = pltpu.get_barrier_semaphore()
    for i in range(3):
        for there, by in ((below[i], -1), (above[i], 1)):
            @pl.when(there)
            def _():
                pl.semaphore_signal(
                    barrier, inc=1, device_id={AXES[i]: place[i] + by}, device_id_type=MESH
                )

    mid_z, mid_y = pl.ds(1, zs), pl.ds(TOP, ys)
    loads = [
        pltpu.make_async_copy(u_in, bar.at[0, mid_z, mid_y], load_sem.at[0]),
        pltpu.make_async_copy(v_in, bar.at[pl.ds(1, 3), mid_z, mid_y], load_sem.at[1]),
        pltpu.make_async_copy(p_in, pp.at[:, mid_z, mid_y], load_sem.at[2]),
        pltpu.make_async_copy(noisy_in, offset, load_sem.at[3]),
        pltpu.make_async_copy(fid_in, gain, load_sem.at[4]),
    ] + [
        pltpu.make_async_copy(q_in.at[Q_FROM[k]], qq.at[k, mid_z, mid_y], load_sem.at[5 + k])
        for k in range(6)
    ]
    for load in loads:
        load.start()

    row = jnp.zeros((zs + 2, 1, xs), jnp.float32)
    layer = jnp.zeros((ys, xs), jnp.float32)

    @pl.when(jnp.logical_not(below[0]))
    def _():
        got_v[...] = layer
        got_p[...] = layer

    @pl.when(jnp.logical_not(above[0]))
    def _():
        got_u[...] = layer
        got_q[...] = layer

    @pl.when(jnp.logical_not(below[1]))
    def _():
        for k in range(3):
            bar[1 + k, :, TOP - 1 : TOP, :] = row
        pp[1, :, TOP - 1 : TOP, :] = row

    @pl.when(jnp.logical_not(above[1]))
    def _():
        bar[0, :, TOP + ys : TOP + ys + 1, :] = row
        for k in (XY, YY, YZ):
            qq[k, :, TOP + ys : TOP + ys + 1, :] = row

    @pl.when(jnp.logical_not(below[2]))
    def _():
        for k in range(3):
            bar[1 + k, 0, TOP : TOP + ys, :] = layer
        pp[2, 0, TOP : TOP + ys, :] = layer

    @pl.when(jnp.logical_not(above[2]))
    def _():
        bar[0, zs + 1, TOP : TOP + ys, :] = layer
        for k in (YZ, ZZ, XZ):
            qq[k, zs + 1, TOP : TOP + ys, :] = layer

    lane = lax.broadcasted_iota(jnp.int32, (8, xs), 1)
    sub = lax.broadcasted_iota(jnp.int32, (8, xs), 0)
    first_lane, last_lane = lane == 0, lane == xs - 1

    def factor(flag):
        return jnp.where(flag, jnp.float32(1), jnp.float32(0))

    up_x = jnp.where(last_lane, factor(above[0]), 1.0)
    lo_x = jnp.where(first_lane, factor(below[0]), 1.0)
    up_y_last = jnp.where(sub == 7, factor(above[1]), 1.0)
    lo_y_first = jnp.where(sub == 0, factor(below[1]), 1.0)

    def flush(later):
        for ref, at, value in later:
            ref[at + (slice(None),)] = value
        later.clear()

    def each(body):
        def turn(j, carry):
            body(2 * j)
            body(2 * j + 1)
            return carry

        lax.fori_loop(0, zs // 2, turn, 0)

    def sweep(body, moves, wanted):
        def turn(j, packed):
            one, two = list(packed[0]), list(packed[1])
            body(jnp.where(j == 0, 0, 2 * j - 1), one, two)
            body(jnp.where(j == 0, zs - 1, 2 * j), one, two)

            @pl.when(jnp.logical_and(wanted, j == 0))
            def _():
                start(moves)

            return tuple(one), tuple(two)

        return lax.fori_loop(0, zs // 2, turn, (nothing, nothing))

    def up_z(z):
        return factor(jnp.logical_or(z < zs - 1, above[2]))

    def lo_z(z):
        return factor(jnp.logical_or(z > 0, below[2]))

    def up_y(b, value):
        return up_y_last * value if b == blocks - 1 else value

    def lo_y(b, value):
        return lo_y_first * value if b == 0 else value

    def next_x(value):
        return jnp.where(last_lane, 0.0, pltpu.roll(value, xs - 1, 1))

    def prev_x(value):
        return jnp.where(first_lane, 0.0, pltpu.roll(value, 1, 1))

    def halo_next_x(got, k, z):
        return jnp.where(last_lane, pltpu.roll(got, xs - 1 - k * zs - z, 1), 0.0)

    def halo_prev_x(got, k, z):
        return jnp.where(first_lane, pltpu.roll(got, xs - 1 - k * zs - z, 1), 0.0)

    def next_y(ref, k, z, b, value):
        if b < blocks - 1:
            return ref[k, z + 1, rows(b, 1), :]
        return jnp.where(sub == 7, 0.0, pltpu.roll(value, 7, 0))

    def prev_y(ref, k, z, b, value):
        if b > 0:
            return ref[k, z + 1, rows(b, -1), :]
        return jnp.where(sub == 0, 0.0, pltpu.roll(value, 1, 0))

    def halo_next_y(ref, k, z, b):
        return jnp.where(sub == 7, ref[k, z + 1, rows(b, 1), :], 0.0)

    def halo_prev_y(ref, k, z, b):
        return jnp.where(sub == 0, ref[k, z + 1, rows(b, -1), :], 0.0)

    def next_z(ref, k, z, b):
        return factor(z < zs - 1) * ref[k, jnp.minimum(z + 2, zs), rows(b), :]

    def prev_z(ref, k, z, b):
        return factor(z > 0) * ref[k, jnp.maximum(z, 1), rows(b), :]

    def pack_first(packed, value, k, z):
        return jnp.where(lane == k * zs + z, pltpu.roll(value, k * zs + z, 1), packed)

    def pack_last(packed, value, k, z):
        return jnp.where(lane == k * zs + z + 1, pltpu.roll(value, k * zs + z + 2, 1), packed)

    def down(src, dst, i, k):
        return (
            pltpu.make_async_remote_copy(
                src_ref=src, dst_ref=dst, send_sem=send_sem.at[k], recv_sem=recv_sem.at[k],
                device_id={AXES[i]: place[i] - 1}, device_id_type=MESH,
            ),
            below[i],
            above[i],
        )

    def up(src, dst, i, k):
        return (
            pltpu.make_async_remote_copy(
                src_ref=src, dst_ref=dst, send_sem=send_sem.at[k], recv_sem=recv_sem.at[k],
                device_id={AXES[i]: place[i] + 1}, device_id_type=MESH,
            ),
            above[i],
            below[i],
        )

    comps = pl.ds(1, 3)
    primal_moves = [
        up(bar.at[comps, zs, mid_y], bar.at[comps, 0, mid_y], 2, 0),
        down(bar.at[0, 1, mid_y], bar.at[0, zs + 1, mid_y], 2, 1),
        up(bar.at[comps, mid_z, TOP + ys - 1], bar.at[comps, mid_z, TOP - 1], 1, 2),
        down(bar.at[0, mid_z, TOP], bar.at[0, mid_z, TOP + ys], 1, 3),
        up(send_v, got_v, 0, 4),
        down(send_u, got_u, 0, 5),
    ]
    dual_moves = [
        down(qq.at[pl.ds(YZ, 3), 1, mid_y], qq.at[pl.ds(YZ, 3), zs + 1, mid_y], 2, 6),
        up(pp.at[2, zs, mid_y], pp.at[2, 0, mid_y], 2, 7),
        down(qq.at[pl.ds(XY, 3), mid_z, TOP], qq.at[pl.ds(XY, 3), mid_z, TOP + ys], 1, 8),
        up(pp.at[1, mid_z, TOP + ys - 1], pp.at[1, mid_z, TOP - 1], 1, 9),
        down(send_q, got_q, 0, 10),
        up(send_p, got_p, 0, 11),
    ]

    def start(moves):
        for copy, goes, comes in moves:
            @pl.when(goes)
            def _():
                copy.start()

    def finish(moves):
        for copy, goes, comes in moves:
            @pl.when(goes)
            def _():
                copy.wait_send()

            @pl.when(comes)
            def _():
                copy.wait_recv()

    empty = jnp.zeros((8, xs), jnp.float32)

    def rows(b, by=0):
        return pl.ds(TOP + 8 * b + by, 8)

    def store_packed(ref, packed):
        for b in range(blocks):
            ref[pl.ds(8 * b, 8), :] = packed[b]

    for load in loads[:2]:
        load.wait()
    pl.semaphore_wait(barrier, peers)
    start(primal_moves[:4])

    def first_faces(z, packed):
        first, last = list(packed[0]), list(packed[1])
        for b in range(blocks):
            first[b] = pack_first(first[b], bar[0, z + 1, rows(b), :], 0, z)
            for k in range(3):
                last[b] = pack_last(last[b], bar[1 + k, z + 1, rows(b), :], k, z)
        return tuple(first), tuple(last)

    nothing = (empty,) * blocks
    first, last = lax.fori_loop(0, zs, first_faces, (nothing, nothing))
    store_packed(send_u, first)
    store_packed(send_v, last)
    start(primal_moves[4:])

    for load in loads[2:]:
        load.wait()

    def prepare(z, carry):
        weight = TAU * gain[z]
        inverse = 1.0 / (1.0 + weight)
        gain[z] = inverse
        offset[z] = weight * offset[z] * inverse
        u_out[z] = bar[0, z + 1, mid_y, :]
        for k in range(3):
            v_out[k, z] = bar[1 + k, z + 1, mid_y, :]
        return carry

    lax.fori_loop(0, zs, prepare, 0)

    def iteration(step, carry):
        more = step < ITERS - 1

        def dual_inside(z):
            later = []
            z_up, z_lo = up_z(z), lo_z(z)
            for b in range(blocks):
                r = rows(b)
                u = bar[0, z + 1, r, :]
                v = [bar[1 + k, z + 1, r, :] for k in range(3)]
                slopes = (
                    next_x(u) - up_x * u,
                    next_y(bar, 0, z, b, u) - up_y(b, u),
                    next_z(bar, 0, z, b) - z_up * u,
                )
                for k in range(3):
                    later.append((pp, (k, z + 1, r), pp[k, z + 1, r, :] + SIGMA * (slopes[k] - v[k])))
                dx = [lo_x * v[k] - prev_x(v[k]) for k in range(3)]
                dy = [lo_y(b, v[k]) - prev_y(bar, 1 + k, z, b, v[k]) for k in range(3)]
                dz = [z_lo * v[k] - prev_z(bar, 1 + k, z, b) for k in range(3)]
                half = 0.5 * SIGMA
                for k, add in (
                    (XX, SIGMA * dx[0]), (YY, SIGMA * dy[1]), (ZZ, SIGMA * dz[2]),
                    (XY, half * (dy[0] + dx[1])), (XZ, half * (dz[0] + dx[2])),
                    (YZ, half * (dz[1] + dy[2])),
                ):
                    later.append((qq, (k, z + 1, r), qq[k, z + 1, r, :] + add))
            flush(later)

        each(dual_inside)
        finish(primal_moves)

        def dual(z, of_p, of_q):
            z_end, z_begin, half = SIGMA * factor(z == zs - 1), factor(z == 0), 0.5 * SIGMA
            later = []
            for b in range(blocks):
                r, here = rows(b), pl.ds(8 * b, 8)
                t = [pp[k, z + 1, r, :] for k in range(3)]
                t[0] = t[0] + SIGMA * halo_next_x(got_u[here, :], 0, z)
                if b == blocks - 1:
                    t[1] = t[1] + SIGMA * halo_next_y(bar, 0, z, b)
                t[2] = t[2] + z_end * bar[0, z + 2, r, :]
                size = t[0] * t[0] + t[1] * t[1] + t[2] * t[2]
                scale = jnp.minimum(1.0, ALPHA1 * lax.rsqrt(size))
                t = [scale * part for part in t]
                for k in range(3):
                    later.append((pp, (k, z + 1, r), t[k]))
                    later.append((p_out, (k, z, here), t[k]))
                of_p[b] = pack_last(of_p[b], t[0], 0, z)

                received = got_v[here, :]
                hx = [halo_prev_x(received, k, z) for k in range(3)]
                hz = [z_begin * bar[1 + k, z, r, :] for k in range(3)]
                s = [qq[k, z + 1, r, :] for k in range(6)]
                s[XX] = s[XX] - SIGMA * hx[0]
                s[ZZ] = s[ZZ] - SIGMA * hz[2]
                s[XZ] = s[XZ] - half * (hz[0] + hx[2])
                if b == 0:
                    hy = [halo_prev_y(bar, 1 + k, z, b) for k in range(3)]
                    s[YY] = s[YY] - SIGMA * hy[1]
                    s[XY] = s[XY] - half * (hy[0] + hx[1])
                    s[YZ] = s[YZ] - half * (hz[1] + hy[2])
                else:
                    s[XY] = s[XY] - half * hx[1]
                    s[YZ] = s[YZ] - half * hz[1]
                size = (s[XX] * s[XX] + s[YY] * s[YY] + s[ZZ] * s[ZZ]) + 2.0 * (
                    s[XY] * s[XY] + s[XZ] * s[XZ] + s[YZ] * s[YZ]
                )
                scale = jnp.minimum(1.0, ALPHA0 * lax.rsqrt(size))
                s = [scale * part for part in s]
                for k in range(6):
                    later.append((qq, (k, z + 1, r), s[k]))
                    later.append((q_out, (Q_FROM[k], z, here), s[k]))
                for k, part in enumerate((XX, XY, XZ)):
                    of_q[b] = pack_first(of_q[b], s[part], k, z)
            flush(later)

        of_p, of_q = sweep(dual, dual_moves[:2], True)
        store_packed(send_p, of_p)
        store_packed(send_q, of_q)
        start(dual_moves[2:])

        parts_of = ((XX, XY, XZ), (XY, YY, YZ), (XZ, YZ, ZZ))

        def primal_inside(z):
            later = []
            z_up, z_lo = up_z(z), lo_z(z)
            for b in range(blocks):
                r, here = rows(b), pl.ds(8 * b, 8)
                p = [pp[k, z + 1, r, :] for k in range(3)]
                div = (
                    (up_x * p[0] - prev_x(p[0]))
                    + (up_y(b, p[1]) - prev_y(pp, 1, z, b, p[1]))
                    + (z_up * p[2] - prev_z(pp, 2, z, b))
                )
                new = (u_out[z, here, :] + TAU * div) * gain[z, here, :] + offset[z, here, :]
                later.append((partial, (0, z, here), new))
                q = [qq[k, z + 1, r, :] for k in range(6)]
                for k, (ax, ay, az) in enumerate(parts_of):
                    div2 = (
                        (next_x(q[ax]) - lo_x * q[ax])
                        + (next_y(qq, ay, z, b, q[ay]) - lo_y(b, q[ay]))
                        + (next_z(qq, az, z, b) - z_lo * q[az])
                    )
                    new = v_out[k, z, here, :] + TAU * (p[k] + div2)
                    later.append((partial, (1 + k, z, here), new))
            flush(later)

        each(primal_inside)
        finish(dual_moves)

        def primal(z, of_u, of_v):
            later = []
            z_end, z_begin = factor(z == zs - 1), factor(z == 0)
            for b in range(blocks):
                r, here = rows(b), pl.ds(8 * b, 8)
                received = got_q[here, :]
                for k, (ax, ay, az) in enumerate(parts_of):
                    halo = halo_next_x(received, k, z) + z_end * qq[az, z + 2, r, :]
                    if b == blocks - 1:
                        halo = halo + halo_next_y(qq, ay, z, b)
                    old = v_out[k, z, here, :]
                    new = partial[1 + k, z, here, :] + TAU * halo
                    later.append((v_out, (k, z, here), new))
                    ahead = 2.0 * new - old
                    later.append((bar, (1 + k, z + 1, r), ahead))
                    of_v[b] = pack_last(of_v[b], ahead, k, z)
                halo = halo_prev_x(got_p[here, :], 0, z) + z_begin * pp[2, z, r, :]
                if b == 0:
                    halo = halo + halo_prev_y(pp, 1, z, b)
                old = u_out[z, here, :]
                new = partial[0, z, here, :] - (TAU * halo) * gain[z, here, :]
                later.append((u_out, (z, here), new))
                ahead = 2.0 * new - old
                later.append((bar, (0, z + 1, r), ahead))
                of_u[b] = pack_first(of_u[b], ahead, 0, z)
            flush(later)

        of_u, of_v = sweep(primal, primal_moves[:2], more)

        @pl.when(more)
        def _():
            store_packed(send_u, of_u)
            store_packed(send_v, of_v)
            start(primal_moves[2:])

        return carry

    lax.fori_loop(0, ITERS, iteration, 0)


def copy_out(u_in, v_in, p_in, q_in, u_out, v_out, p_out, q_out, sems):
    pairs = ((q_in, q_out), (p_in, p_out), (v_in, v_out), (u_in, u_out))
    copies = [pltpu.make_async_copy(a, b, sems.at[i]) for i, (a, b) in enumerate(pairs)]
    for copy in copies:
        copy.start()
    for copy in copies:
        copy.wait()


def per_device(noisy_image, fidelity, primal_u, primal_v, dual_p, dual_q):
    zs, ys, xs = primal_u.shape
    assert xs == 128 and ys % 8 == 0 and zs % 2 == 0 and 3 * zs < xs
    f32 = jnp.float32
    padded = (zs + 2, ys + 2 * TOP, xs)
    face = pltpu.VMEM((ys, xs), f32)
    results = pl.pallas_call(
        kernel,
        out_shape=tuple(pltpu.VMEM(a.shape, f32) for a in (primal_u, primal_v, dual_p, dual_q)),
        in_specs=[pl.BlockSpec(memory_space=pl.ANY)] * 6,
        out_specs=tuple([pl.BlockSpec(memory_space=pltpu.VMEM)] * 4),
        scratch_shapes=[
            pltpu.VMEM((4,) + padded, f32),
            pltpu.VMEM((3,) + padded, f32),
            pltpu.VMEM((6,) + padded, f32),
            pltpu.VMEM((zs, ys, xs), f32),
            pltpu.VMEM((zs, ys, xs), f32),
            pltpu.VMEM((4, zs, ys, xs), f32),
        ]
        + [face] * 8
        + [
            pltpu.SemaphoreType.DMA((11,)),
            pltpu.SemaphoreType.DMA((12,)),
            pltpu.SemaphoreType.DMA((12,)),
        ],
        compiler_params=pltpu.CompilerParams(collective_id=0, has_side_effects=True),
        name="tgv",
    )(noisy_image, fidelity, primal_u, primal_v, dual_p, dual_q)
    return pl.pallas_call(
        copy_out,
        out_shape=tuple(jax.ShapeDtypeStruct(a.shape, f32) for a in results),
        in_specs=[pl.BlockSpec(memory_space=pltpu.VMEM)] * 4,
        out_specs=tuple([pl.BlockSpec(memory_space=pl.ANY)] * 4),
        scratch_shapes=[pltpu.SemaphoreType.DMA((4,))],
        name="out",
    )(*[pltpu.with_memory_space_constraint(r, pltpu.VMEM) for r in results])


def solution(mesh):
    scalar, stack = P("gz", "gy", "gx"), P(None, "gz", "gy", "gx")
    return jax.shard_map(
        per_device,
        mesh=mesh,
        in_specs=(scalar, scalar, scalar, stack, stack, stack),
        out_specs=(scalar, stack, stack, stack),
        check_vma=False,
    )
```

profile of v0, /device:TPU:0, one launch (start us, length us, event | category | flops | bytes accessed | tf_op | source)
XLA Modules:
  0.0 28.0 jit_solution(2761717622417301995)
XLA Ops:
  0.6 26.2 %tgv.1 = (f32[8,32,128]{2,1,0:T(8,128)S(1)}, f32[3,8,32,128]{3,2,1,0:T(8,128)S(1)}, f32[3,8,32,128]{3,2,1,0:T(8,128)S(1)}, f32[6,8,32,128]{3,2,1,0:T(8,128)S(1)}) custom-call(f32[8,32,128]{2,1,0:T(8,128)} %noisy_in.1, f32[8,32,128]{2,1,0:T(8,128)} %fid_in.1, f32[8,32,128]{2,1,0:T(8,128)} %u_in.1, f32[3,8,32,128]{3,2,1,0:T(8,128)} %v_in.1, ...), custom_call_target="tpu_custom_call" | custom-call | tf_op jit(solution)/shard_map/tgv/pallas_call | solution.py:450
  26.8 1.2 %out.1 = (f32[8,32,128]{2,1,0:T(8,128)}, f32[3,8,32,128]{3,2,1,0:T(8,128)}, f32[3,8,32,128]{3,2,1,0:T(8,128)}, f32[6,8,32,128]{3,2,1,0:T(8,128)}) custom-call(f32[8,32,128]{2,1,0:T(8,128)S(1)} %get-tuple-element.8.u_in, f32[3,8,32,128]{3,2,1,0:T(8,128)S(1)} %get-tuple-element.9.v_in, f32[3,8,32,128]{3,2,1,0:T(8,128)S(1)} %get-tuple-element.10.p_in, ...), custom_call_target="tpu_custom_call" | custom-call | tf_op jit(solution)/shard_map/out/pallas_call | solution.py:472
where the time goes:
time: 28.2 us; the launch traced here: 28 us
  Pallas kernels  27.4 us (97%)
  between operations  0.64 us (2%)
    pallas_call x1, Pallas kernels, per_device(): pl.pallas_call(kernel, out_shape=tuple((pltpu.VMEM(a.shape, f32) for a in...  26.2 us
    pallas_call x1, Pallas kernels, per_device(): pl.pallas_call(copy_out, out_shape=tuple((jax.ShapeDtypeStruct(a.shape, f...  1.21 us

commit v1 on v0

v1 whole, which is shorter than its diff:
```python
import jax
import jax.numpy as jnp
from jax import lax
from jax.experimental import pallas as pl
from jax.experimental.pallas import tpu as pltpu
from jax.sharding import PartitionSpec as P

ITERS = 3
AXES = ("gx", "gy", "gz")
ALPHA1, ALPHA0, SIGMA, TAU = 0.5, 1.0, 0.2, 0.2
XX, YY, ZZ, XY, XZ, YZ = range(6)
PARTS = ((XX, XY, XZ), (XY, YY, YZ), (XZ, YZ, ZZ))
MESH = pl.DeviceIdType.MESH
Z_UP, Z_DOWN, X_UP, X_DOWN, Y_UP, Y_DOWN, XY_A, XY_B, XZ_A, XZ_B, YZ_A, YZ_B = range(12)
WAYS = (
    (0, 0, 1), (0, 0, -1), (1, 0, 0), (-1, 0, 0), (0, 1, 0), (0, -1, 0),
    (1, -1, 0), (-1, 1, 0), (1, 0, -1), (-1, 0, 1), (0, 1, -1), (0, -1, 1),
)


def kernel(
    noisy_in, fid_in, u_in, v_in, p_in, q_in,
    u_out, v_out, p_out, q_out,
    bar, gain, offset, face,
    z_lo, z_hi, x_lo, x_hi, y_lo, y_hi, d_a, d_b, d_c, d_d, d_e, d_g,
    zp, zq, yp, yq, xs_own, xp, xq, cv, cp,
    load_sem, send_sem, recv_sem, first_send, first_recv,
):
    zs, ys, xs = u_in.shape
    blocks = ys // 8
    pairs = zs * blocks
    half_lanes = 2 * pairs
    place = [lax.axis_index(a) for a in AXES]
    count = [lax.axis_size(a) for a in AXES]
    below = [place[i] > 0 for i in range(3)]
    above = [place[i] < count[i] - 1 for i in range(3)]

    def exists(way):
        there = None
        for i, by in enumerate(way):
            if by:
                one = above[i] if by > 0 else below[i]
                there = one if there is None else jnp.logical_and(there, one)
        return there

    def target(way):
        return {AXES[i]: place[i] + by for i, by in enumerate(way) if by}

    goes = [exists(way) for way in WAYS]
    comes = [exists(tuple(-by for by in way)) for way in WAYS]
    peers = sum(there.astype(jnp.int32) for there in goes)

    barrier = pltpu.get_barrier_semaphore()
    for way, there in zip(WAYS, goes):
        @pl.when(there)
        def _():
            pl.semaphore_signal(barrier, inc=1, device_id=target(way), device_id_type=MESH)

    u_face, xf, top_face = pl.ds(0, 4), pl.ds(4, 2), pl.ds(6, 4)
    loads = [
        pltpu.make_async_copy(u_in, bar.at[0], load_sem.at[0]),
        pltpu.make_async_copy(v_in, bar.at[pl.ds(1, 3)], load_sem.at[1]),
        pltpu.make_async_copy(u_in.at[:, 0], face.at[0], load_sem.at[2]),
        pltpu.make_async_copy(v_in.at[:, :, 0], face.at[pl.ds(1, 3)], load_sem.at[3]),
        pltpu.make_async_copy(u_in.at[:, ys - 1], face.at[6], load_sem.at[4]),
        pltpu.make_async_copy(v_in.at[:, :, ys - 1], face.at[pl.ds(7, 3)], load_sem.at[5]),
        pltpu.make_async_copy(p_in, p_out, load_sem.at[6]),
        pltpu.make_async_copy(q_in, q_out, load_sem.at[7]),
        pltpu.make_async_copy(noisy_in, offset, load_sem.at[8]),
        pltpu.make_async_copy(fid_in, gain, load_sem.at[9]),
        pltpu.make_async_copy(u_in, u_out, load_sem.at[10]),
        pltpu.make_async_copy(v_in, v_out, load_sem.at[11]),
    ]
    for load in loads:
        load.start()

    def clear(there, *refs):
        @pl.when(jnp.logical_not(there))
        def _():
            for ref in refs:
                ref[...] = jnp.zeros(ref.shape, jnp.float32)

    clear(below[0], x_lo, xp)
    clear(above[0], x_hi, xq)
    clear(below[1], y_lo, yp)
    clear(above[1], y_hi, yq)
    clear(below[2], z_lo, zp)
    clear(above[2], z_hi, zq)
    for way, ref in zip(WAYS[6:], (d_a, d_b, d_c, d_d, d_e, d_g)):
        clear(exists(tuple(-by for by in way)), ref)

    lane = lax.broadcasted_iota(jnp.int32, (8, xs), 1)
    sub = lax.broadcasted_iota(jnp.int32, (8, xs), 0)
    pair = lane >> 1
    odd = (lane & 1) == 1
    first_lane, last_lane = lane == 0, lane == xs - 1
    first_row, last_row = sub == 0, sub == 7
    of_block = pair & (blocks - 1)
    first_block, last_block = of_block == 0, of_block == blocks - 1
    first_z, last_z = pair < blocks, jnp.logical_and(pair >= pairs - blocks, pair < pairs)

    def factor(flag):
        return jnp.where(flag, jnp.float32(1), jnp.float32(0))

    up_x = jnp.where(last_lane, factor(above[0]), 1.0)
    lo_x = jnp.where(first_lane, factor(below[0]), 1.0)
    up_y_last = jnp.where(last_row, factor(above[1]), 1.0)
    lo_y_first = jnp.where(first_row, factor(below[1]), 1.0)

    def rows(b, by=0):
        return pl.ds(8 * b + by, 8)

    def turn_lanes(value, by):
        return value if isinstance(by, int) and by % xs == 0 else pltpu.roll(value, by % xs if isinstance(by, int) else by, 1)

    def turn_rows(value, by):
        return pltpu.roll(value, by % 8, 0)

    def flush(later):
        for ref, at, value in later:
            ref[at + (slice(None),)] = value
        later.clear()

    def up_z(z):
        return factor(jnp.logical_or(z < zs - 1, above[2]))

    def lo_z(z):
        return factor(jnp.logical_or(z > 0, below[2]))

    def up_y(b, value):
        return up_y_last * value if b == blocks - 1 else value

    def lo_y(b, value):
        return lo_y_first * value if b == 0 else value

    def next_x(value):
        return jnp.where(last_lane, 0.0, pltpu.roll(value, xs - 1, 1))

    def prev_x(value):
        return jnp.where(first_lane, 0.0, pltpu.roll(value, 1, 1))

    def next_y(ref, k, z, b, value):
        if b < blocks - 1:
            return ref[k, z, rows(b, 1), :]
        return jnp.where(last_row, 0.0, pltpu.roll(value, 7, 0))

    def prev_y(ref, k, z, b, value):
        if b > 0:
            return ref[k, z, rows(b, -1), :]
        return jnp.where(first_row, 0.0, pltpu.roll(value, 1, 0))

    def next_z(ref, k, z, b):
        if isinstance(z, int):
            return ref[k, z + 1, rows(b), :] if z < zs - 1 else jnp.zeros((8, xs), jnp.float32)
        return factor(z < zs - 1) * ref[k, jnp.minimum(z + 1, zs - 1), rows(b), :]

    def prev_z(ref, k, z, b):
        if isinstance(z, int):
            return ref[k, z - 1, rows(b), :] if z > 0 else jnp.zeros((8, xs), jnp.float32)
        return factor(z > 0) * ref[k, jnp.maximum(z - 1, 0), rows(b), :]

    def shrink_p(t):
        size = t[0] * t[0] + t[1] * t[1] + t[2] * t[2]
        scale = jnp.minimum(1.0, ALPHA1 * lax.rsqrt(size))
        return [scale * part for part in t]

    def shrink_q(s):
        size = (s[XX] * s[XX] + s[YY] * s[YY] + s[ZZ] * s[ZZ]) + 2.0 * (
            s[XY] * s[XY] + s[XZ] * s[XZ] + s[YZ] * s[YZ]
        )
        scale = jnp.minimum(1.0, ALPHA0 * lax.rsqrt(size))
        return [scale * part for part in s]

    half = 0.5 * SIGMA

    def grow_q(q, dx, dy, dz):
        return [
            q[XX] + SIGMA * dx[0], q[YY] + SIGMA * dy[1], q[ZZ] + SIGMA * dz[2],
            q[XY] + half * (dy[0] + dx[1]), q[XZ] + half * (dz[0] + dx[2]),
            q[YZ] + half * (dz[1] + dy[2]),
        ]

    def keep(flag, value):
        return jnp.where(flag, value, 0.0)

    def pack(packed, value, base, j):
        return jnp.where(pair == base + j, pltpu.roll(value, 2 * (base + j) + 1, 1), packed)

    def pack_bar(packed, values, z, b):
        j = z * blocks + b
        packed[0] = pack(packed[0], values[0], 0, j)
        packed[0] = pack(packed[0], values[1], pairs, j)
        packed[1] = pack(packed[1], values[2], 0, j)
        packed[1] = pack(packed[1], values[3], pairs, j)

    def message(src, dst, way, send, recv):
        return pltpu.make_async_remote_copy(
            src_ref=src, dst_ref=dst, send_sem=send, recv_sem=recv,
            device_id=target(WAYS[way]), device_id_type=MESH,
        )

    exchanges = []
    for s in range(ITERS):
        ends = (
            (bar.at[:, zs - 1], z_lo.at[s]),
            (bar.at[:, 0], z_hi.at[s]),
            (face.at[xf], x_lo.at[s]),
            (face.at[xf], x_hi.at[s]),
            (face.at[top_face], y_lo.at[s]),
            (face.at[u_face], y_hi.at[s]),
            (face.at[pl.ds(0, 6)], d_a.at[s]),
            (face.at[pl.ds(4, 6)], d_b.at[s]),
            (face.at[xf], d_c.at[s]),
            (face.at[xf], d_d.at[s]),
            (face.at[top_face, pl.ds(0, 1)], d_e.at[s, :, pl.ds(0, 1)]),
            (face.at[u_face, pl.ds(zs - 1, 1)], d_g.at[s, :, pl.ds(zs - 1, 1)]),
        )
        exchanges.append([
            (message(src, dst, k, send_sem.at[s, k], recv_sem.at[s, k]), goes[k], comes[k])
            for k, (src, dst) in enumerate(ends)
        ])
    duals = [
        (message(src, dst, way, first_send.at[k], first_recv.at[k]), goes[way], comes[way])
        for k, (src, dst, way) in enumerate((
            (p_in.at[:, zs - 1], zp, Z_UP),
            (q_in.at[:, 0], zq, Z_DOWN),
            (p_in.at[:, :, ys - 1], yp, Y_UP),
            (q_in.at[:, :, 0], yq, Y_DOWN),
            (xs_own, xp, X_UP),
            (xs_own, xq, X_DOWN),
        ))
    ]

    def start(moves):
        for copy, there, _ in moves:
            @pl.when(there)
            def _():
                copy.start()

    def sent(moves):
        for copy, there, _ in moves:
            @pl.when(there)
            def _():
                copy.wait_send()

    def got(moves):
        for copy, _, there in moves:
            @pl.when(there)
            def _():
                copy.wait_recv()

    empty = jnp.zeros((8, xs), jnp.float32)

    def each(low, high, body, carry):
        def turn(j, carry):
            one = list(carry)
            body(low + 2 * j, one)
            body(low + 2 * j + 1, one)
            return tuple(one)

        return lax.fori_loop(0, (high - low) // 2, turn, tuple(carry))

    def dual_inside(z, _):
        later = []
        z_up, z_lo_ = up_z(z), lo_z(z)
        for b in range(blocks):
            r = rows(b)
            u = bar[0, z, r, :]
            v = [bar[1 + k, z, r, :] for k in range(3)]
            slopes = (
                next_x(u) - up_x * u,
                next_y(bar, 0, z, b, u) - up_y(b, u),
                next_z(bar, 0, z, b) - z_up * u,
            )
            for k in range(3):
                later.append((p_out, (k, z, r), p_out[k, z, r, :] + SIGMA * (slopes[k] - v[k])))
            dx = [lo_x * v[k] - prev_x(v[k]) for k in range(3)]
            dy = [lo_y(b, v[k]) - prev_y(bar, 1 + k, z, b, v[k]) for k in range(3)]
            dz = [z_lo_ * v[k] - prev_z(bar, 1 + k, z, b) for k in range(3)]
            for k, new in enumerate(grow_q([q_out[k, z, r, :] for k in range(6)], dx, dy, dz)):
                later.append((q_out, (k, z, r), new))
        flush(later)

    def line_up(s):
        cv[0] = jnp.where(odd, turn_lanes(x_hi[s, 0], half_lanes - 2), x_lo[s, 0])
        cv[1] = turn_lanes(x_lo[s, 1], half_lanes)
        cv[2] = x_lo[s, 1]

    def dual(z, s):
        later = []
        for b in range(blocks):
            r = rows(b)
            by = half_lanes - 2 * (z * blocks + b)
            from_x = [turn_lanes(cv[k], by) for k in range(3)]
            t = [p_out[k, z, r, :] for k in range(3)]
            t[0] = t[0] + SIGMA * jnp.where(last_lane, from_x[0], 0.0)
            if b == blocks - 1:
                t[1] = t[1] + SIGMA * jnp.where(last_row, y_hi[s, 0, pl.ds(z, 1), :], 0.0)
            if isinstance(z, int) and z == zs - 1:
                t[2] = t[2] + SIGMA * z_hi[s, 0, r, :]
            for k, new in enumerate(shrink_p(t)):
                later.append((p_out, (k, z, r), new))
            hx = [jnp.where(first_lane, part, 0.0) for part in from_x]
            q = [q_out[k, z, r, :] for k in range(6)]
            q[XX] = q[XX] - SIGMA * hx[0]
            q[XY] = q[XY] - half * hx[1]
            q[XZ] = q[XZ] - half * hx[2]
            if b == 0:
                hy = [jnp.where(first_row, y_lo[s, 1 + k, pl.ds(z, 1), :], 0.0) for k in range(3)]
                q[YY] = q[YY] - SIGMA * hy[1]
                q[XY] = q[XY] - half * hy[0]
                q[YZ] = q[YZ] - half * hy[2]
            if isinstance(z, int) and z == 0:
                hz = [z_lo[s, 1 + k, r, :] for k in range(3)]
                q[ZZ] = q[ZZ] - SIGMA * hz[2]
                q[XZ] = q[XZ] - half * hz[0]
                q[YZ] = q[YZ] - half * hz[1]
            for k, new in enumerate(shrink_q(q)):
                later.append((q_out, (k, z, r), new))
        flush(later)

    def halo_x(s):
        own = [face[4], face[5]]
        up_yc = jnp.where(jnp.logical_and(last_row, last_block), factor(above[1]), 1.0)
        lo_yc = jnp.where(jnp.logical_and(first_row, first_block), factor(below[1]), 1.0)
        up_zc = jnp.where(last_z, factor(above[2]), 1.0)
        lo_zc = jnp.where(first_z, factor(below[2]), 1.0)
        got0, got1 = x_lo[s, 0], x_lo[s, 1]
        u = got0
        v = [turn_lanes(got0, half_lanes), got1, turn_lanes(got1, half_lanes)]
        moved = turn_rows(u, -1)
        edge_y = turn_lanes(turn_rows(d_a[s, 4], -1), 2 * (blocks - 1))
        ahead_y = jnp.where(last_row, jnp.where(last_block, edge_y, turn_lanes(moved, -2)), moved)
        ahead_z = jnp.where(
            last_z, turn_lanes(d_c[s, 0], half_lanes - 2 * blocks), turn_lanes(u, -2 * blocks)
        )
        slopes = (turn_lanes(own[0], -1) - u, ahead_y - up_yc * u, ahead_z - up_zc * u)
        p = shrink_p([xp[k] + SIGMA * (slopes[k] - v[k]) for k in range(3)])
        p = [keep(below[0], part) for part in p]

        got0, got1 = x_hi[s, 0], x_hi[s, 1]
        v = [turn_lanes(got0, half_lanes), got1, turn_lanes(got1, half_lanes)]
        mine = [turn_lanes(own[0], half_lanes + 1), turn_lanes(own[1], 1), turn_lanes(own[1], half_lanes + 1)]
        where = ((0, half_lanes), (1, 0), (1, half_lanes))
        dx, dy, dz = [], [], []
        for k, (h, base) in enumerate(where):
            dx.append(v[k] - mine[k])
            moved = turn_rows(v[k], 1)
            edge_y = turn_lanes(turn_rows(d_b[s, h], 1), -base - 2 * (blocks - 1))
            behind_y = jnp.where(first_row, jnp.where(first_block, edge_y, turn_lanes(moved, 2)), moved)
            dy.append(lo_yc * v[k] - behind_y)
            edge_z = turn_lanes(d_d[s, h], -base - 2 * blocks * (zs - 1))
            dz.append(lo_zc * v[k] - jnp.where(first_z, edge_z, turn_lanes(v[k], 2 * blocks)))
        q = shrink_q(grow_q([xq[k] for k in range(6)], dx, dy, dz))
        q = [keep(above[0], part) for part in q]
        for k in range(3):
            xp[k] = p[k]
        for k in range(6):
            xq[k] = q[k]
        cp[0] = jnp.where(odd, turn_lanes(q[XX], half_lanes - 2), turn_lanes(p[0], half_lanes))
        cp[1] = turn_lanes(q[XY], half_lanes - 2)
        cp[2] = turn_lanes(q[XZ], half_lanes - 2)

    def halo_y(s):
        up_zr = jnp.where(last_row, factor(above[2]), 1.0)
        lo_zr = jnp.where(first_row, factor(below[2]), 1.0)
        u = y_lo[s, 0]
        slopes = (
            turn_lanes(jnp.where(first_lane, d_b[s, 2], u), -1) - up_x * u,
            face[0] - u,
            jnp.where(last_row, d_e[s, 0, pl.ds(0, 1), :], turn_rows(u, -1)) - up_zr * u,
        )
        p = shrink_p([yp[k] + SIGMA * (slopes[k] - y_lo[s, 1 + k]) for k in range(3)])
        v = [y_hi[s, 1 + k] for k in range(3)]
        dx = [lo_x * v[k] - turn_lanes(jnp.where(last_lane, d_a[s, 1 + k], v[k]), 1) for k in range(3)]
        dy = [v[k] - face[7 + k] for k in range(3)]
        dz = [
            lo_zr * v[k] - jnp.where(first_row, d_g[s, 1 + k, pl.ds(zs - 1, 1), :], turn_rows(v[k], 1))
            for k in range(3)
        ]
        q = shrink_q(grow_q([yq[k] for k in range(6)], dx, dy, dz))
        for k in range(3):
            yp[k] = keep(below[1], p[k])
        for k in range(6):
            yq[k] = keep(above[1], q[k])

    def halo_z(s):
        later = []
        for b in range(blocks):
            r = rows(b)
            u = z_lo[s, 0, r, :]
            edge_x = turn_lanes(d_d[s, 0], xs - 2 - 2 * (blocks * (zs - 1) + b))
            if b < blocks - 1:
                ahead_y = z_lo[s, 0, rows(b, 1), :]
            else:
                ahead_y = jnp.where(last_row, d_g[s, 0, pl.ds(zs - 1, 1), :], turn_rows(u, -1))
            slopes = (
                jnp.where(last_lane, edge_x, turn_lanes(u, -1)) - up_x * u,
                ahead_y - up_y(b, u),
                bar[0, 0, r, :] - u,
            )
            p = shrink_p([zp[k, r, :] + SIGMA * (slopes[k] - z_lo[s, 1 + k, r, :]) for k in range(3)])
            for k in range(3):
                later.append((zp, (k, r), keep(below[2], p[k])))

            v = [z_hi[s, 1 + k, r, :] for k in range(3)]
            where = ((0, half_lanes), (1, 0), (1, half_lanes))
            dx, dy, dz = [], [], []
            for k, (h, base) in enumerate(where):
                edge_x = turn_lanes(d_c[s, h], -base - 2 * b)
                dx.append(lo_x * v[k] - jnp.where(first_lane, edge_x, turn_lanes(v[k], 1)))
                if b > 0:
                    behind_y = z_hi[s, 1 + k, rows(b, -1), :]
                else:
                    behind_y = jnp.where(first_row, d_e[s, 1 + k, pl.ds(0, 1), :], turn_rows(v[k], 1))
                dy.append(lo_y(b, v[k]) - behind_y)
                dz.append(v[k] - bar[1 + k, zs - 1, r, :])
            q = shrink_q(grow_q([zq[k, r, :] for k in range(6)], dx, dy, dz))
            for k in range(6):
                later.append((zq, (k, r), keep(above[2], q[k])))
        flush(later)

    def primal(z, packed, last):
        later = []
        z_up, z_lo_ = up_z(z), lo_z(z)
        at_start = isinstance(z, int) and z == 0
        at_end = isinstance(z, int) and z == zs - 1
        for b in range(blocks):
            r = rows(b)
            by = half_lanes - 2 * (z * blocks + b)
            from_x = [turn_lanes(cp[k], by) for k in range(3)]
            p = [p_out[k, z, r, :] for k in range(3)]
            before_x = jnp.where(first_lane, from_x[0], pltpu.roll(p[0], 1, 1))
            if b > 0:
                before_y = p_out[1, z, rows(b, -1), :]
            else:
                before_y = jnp.where(first_row, yp[1, pl.ds(z, 1), :], pltpu.roll(p[1], 1, 0))
            before_z = zp[2, r, :] if at_start else p_out[2, z - 1, r, :]
            div = (up_x * p[0] - before_x) + (up_y(b, p[1]) - before_y) + (z_up * p[2] - before_z)
            old = u_out[z, r, :]
            new = (old + TAU * div) * gain[z, r, :] + offset[z, r, :]
            later.append((u_out, (z, r), new))
            ahead = [2.0 * new - old]
            q = [q_out[k, z, r, :] for k in range(6)]
            for k, (ax, ay, az) in enumerate(PARTS):
                after_x = jnp.where(last_lane, from_x[k], pltpu.roll(q[ax], xs - 1, 1))
                if b < blocks - 1:
                    after_y = q_out[ay, z, rows(b, 1), :]
                else:
                    after_y = jnp.where(last_row, yq[ay, pl.ds(z, 1), :], pltpu.roll(q[ay], 7, 0))
                after_z = zq[az, r, :] if at_end else q_out[az, z + 1, r, :]
                div2 = (
                    (after_x - lo_x * q[ax]) + (after_y - lo_y(b, q[ay])) + (after_z - z_lo_ * q[az])
                )
                old = v_out[k, z, r, :]
                new = old + TAU * (p[k] + div2)
                later.append((v_out, (k, z, r), new))
                ahead.append(2.0 * new - old)
            if not last:
                for k in range(4):
                    later.append((bar, (k, z, r), ahead[k]))
                    if b == 0:
                        later.append((face, (k, pl.ds(z, 1)), ahead[k][0:1, :]))
                    if b == blocks - 1:
                        later.append((face, (6 + k, pl.ds(z, 1)), ahead[k][7:8, :]))
                pack_bar(packed, ahead, z, b)
        flush(later)

    for load in loads[:2]:
        load.wait()
    pl.semaphore_wait(barrier, peers)
    start(exchanges[0][:2])
    start(duals[:4])
    for load in loads[2:6]:
        load.wait()
    start(exchanges[0][4:6])

    def first_faces(z, packed):
        for b in range(blocks):
            pack_bar(packed, [bar[k, z, rows(b), :] for k in range(4)], z, b)

    packed = each(0, zs, first_faces, (empty, empty))
    face[4] = packed[0]
    face[5] = packed[1]
    start(exchanges[0][2:4])
    start(exchanges[0][6:])

    for load in loads[6:8]:
        load.wait()

    def dual_faces(z, packed):
        for b in range(blocks):
            for k in range(6):
                value = q_out[k, z, rows(b), :]
                if k < 3:
                    value = jnp.where(last_lane, p_out[k, z, rows(b), :], value)
                packed[k] = pack(packed[k], value, 0, z * blocks + b)

    for k, value in enumerate(each(0, zs, dual_faces, (empty,) * 6)):
        xs_own[k] = value
    start(duals[4:])

    for load in loads[8:]:
        load.wait()

    def prepare(z, carry):
        weight = TAU * gain[z]
        inverse = 1.0 / (1.0 + weight)
        gain[z] = inverse
        offset[z] = weight * offset[z] * inverse
        return carry

    lax.fori_loop(0, zs, prepare, 0)

    def two_faces(body, carry):
        for z in (0, zs - 1):
            body(z, carry)

    for s in range(ITERS):
        last = s == ITERS - 1
        moves = exchanges[s]
        each(0, zs, dual_inside, ())
        got(moves[2:6])
        line_up(s)
        each(1, zs - 1, lambda z, _: dual(z, s), ())
        got(moves[6:])
        if s == 0:
            got(duals[2:])
        halo_x(s)
        halo_y(s)
        sent(moves[2:])
        packed = list(each(2, zs - 2, lambda z, packed: primal(z, packed, last), (empty, empty)))
        got(moves[:2])
        sent(moves[:2])
        if s == 0:
            got(duals[:2])
            sent(duals)
        halo_z(s)
        for z in (0, zs - 1):
            dual(z, s)
        for z in (0, zs - 1):
            primal(z, packed, last)
        if not last:
            start(exchanges[s + 1][:2])
        for z in (1, zs - 2):
            primal(z, packed, last)
        if not last:
            face[4] = packed[0]
            face[5] = packed[1]
            start(exchanges[s + 1][2:])


def copy_out(u_in, v_in, p_in, q_in, u_out, v_out, p_out, q_out, sems):
    pairs = ((q_in, q_out), (p_in, p_out), (v_in, v_out), (u_in, u_out))
    copies = [pltpu.make_async_copy(a, b, sems.at[i]) for i, (a, b) in enumerate(pairs)]
    for copy in copies:
        copy.start()
    for copy in copies:
        copy.wait()


def per_device(noisy_image, fidelity, primal_u, primal_v, dual_p, dual_q):
    zs, ys, xs = primal_u.shape
    blocks = ys // 8
    assert zs == 8 and ys % 8 == 0 and blocks & (blocks - 1) == 0 and 4 * zs * blocks == xs == 128
    f32 = jnp.float32

    def vmem(*shape):
        return pltpu.VMEM(shape, f32)

    results = pl.pallas_call(
        kernel,
        out_shape=tuple(pltpu.VMEM(a.shape, f32) for a in (primal_u, primal_v, dual_p, dual_q)),
        in_specs=[pl.BlockSpec(memory_space=pl.ANY)] * 6,
        out_specs=tuple([pl.BlockSpec(memory_space=pltpu.VMEM)] * 4),
        scratch_shapes=[
            vmem(4, zs, ys, xs),
            vmem(zs, ys, xs),
            vmem(zs, ys, xs),
            vmem(10, 8, xs),
            vmem(ITERS, 4, ys, xs),
            vmem(ITERS, 4, ys, xs),
            vmem(ITERS, 2, 8, xs),
            vmem(ITERS, 2, 8, xs),
            vmem(ITERS, 4, 8, xs),
            vmem(ITERS, 4, 8, xs),
            vmem(ITERS, 6, 8, xs),
            vmem(ITERS, 6, 8, xs),
            vmem(ITERS, 2, 8, xs),
            vmem(ITERS, 2, 8, xs),
            vmem(ITERS, 4, 8, xs),
            vmem(ITERS, 4, 8, xs),
            vmem(3, ys, xs),
            vmem(6, ys, xs),
            vmem(3, 8, xs),
            vmem(6, 8, xs),
            vmem(6, 8, xs),
            vmem(6, 8, xs),
            vmem(6, 8, xs),
            vmem(3, 8, xs),
            vmem(3, 8, xs),
            pltpu.SemaphoreType.DMA((12,)),
            pltpu.SemaphoreType.DMA((ITERS, 12)),
            pltpu.SemaphoreType.DMA((ITERS, 12)),
            pltpu.SemaphoreType.DMA((6,)),
            pltpu.SemaphoreType.DMA((6,)),
        ],
        compiler_params=pltpu.CompilerParams(collective_id=0, has_side_effects=True),
        name="tgv",
    )(noisy_image, fidelity, primal_u, primal_v, dual_p, dual_q)
    return pl.pallas_call(
        copy_out,
        out_shape=tuple(jax.ShapeDtypeStruct(a.shape, f32) for a in results),
        in_specs=[pl.BlockSpec(memory_space=pltpu.VMEM)] * 4,
        out_specs=tuple([pl.BlockSpec(memory_space=pl.ANY)] * 4),
        scratch_shapes=[pltpu.SemaphoreType.DMA((4,))],
        name="out",
    )(*[pltpu.with_memory_space_constraint(r, pltpu.VMEM) for r in results])


def solution(mesh):
    scalar, stack = P("gz", "gy", "gx"), P(None, "gz", "gy", "gx")
    return jax.shard_map(
        per_device,
        mesh=mesh,
        in_specs=(scalar, scalar, scalar, stack, stack, stack),
        out_specs=(scalar, stack, stack, stack),
        check_vma=False,
    )
```

time: 28.2 us -> 22.9 us (0.81)
  Pallas kernels: 27.4 us -> 22.1 us
    pallas_call x1, Pallas kernels: 26.2 us -> 20.9 us  [per_device(): pl.pallas_call(kernel, out_shape=tuple((pltpu.VMEM(a.shape, f32) for a in...]
where the time goes in v1:
time: 22.9 us; the launch traced here: 22.8 us
  Pallas kernels  22.1 us (97%)
  between operations  0.64 us (3%)
    pallas_call x1, Pallas kernels, per_device(): pl.pallas_call(kernel, out_shape=tuple((pltpu.VMEM(a.shape, f32) for a in...  20.9 us
    pallas_call x1, Pallas kernels, per_device(): pl.pallas_call(copy_out, out_shape=tuple((jax.ShapeDtypeStruct(a.shape, f...  1.21 us

profile of v1, /device:TPU:0, one launch (start us, length us, event | category | flops | bytes accessed | tf_op | source)
XLA Modules:
  0.0 22.8 jit_solution(3503413535813294880)
XLA Ops:
  0.6 20.9 %tgv.1 = (f32[8,32,128]{2,1,0:T(8,128)S(1)}, f32[3,8,32,128]{3,2,1,0:T(8,128)S(1)}, f32[3,8,32,128]{3,2,1,0:T(8,128)S(1)}, f32[6,8,32,128]{3,2,1,0:T(8,128)S(1)}) custom-call(f32[8,32,128]{2,1,0:T(8,128)} %noisy_in.1, f32[8,32,128]{2,1,0:T(8,128)} %fid_in.1, f32[8,32,128]{2,1,0:T(8,128)} %u_in.1, f32[3,8,32,128]{3,2,1,0:T(8,128)} %v_in.1, ...), custom_call_target="tpu_custom_call" | custom-call | tf_op jit(solution)/shard_map/tgv/pallas_call | solution.py:571
  21.6 1.2 %out.1 = (f32[8,32,128]{2,1,0:T(8,128)}, f32[3,8,32,128]{3,2,1,0:T(8,128)}, f32[3,8,32,128]{3,2,1,0:T(8,128)}, f32[6,8,32,128]{3,2,1,0:T(8,128)}) custom-call(f32[8,32,128]{2,1,0:T(8,128)S(1)} %get-tuple-element.8.u_in, f32[3,8,32,128]{3,2,1,0:T(8,128)S(1)} %get-tuple-element.9.v_in, f32[3,8,32,128]{3,2,1,0:T(8,128)S(1)} %get-tuple-element.10.p_in, ...), custom_call_target="tpu_custom_call" | custom-call | tf_op jit(solution)/shard_map/out/pallas_call | solution.py:611

commit v2 on v1

--- a/solution.py
+++ b/solution.py
@@ -50,12 +50,6 @@
     comes = [exists(tuple(-by for by in way)) for way in WAYS]
     peers = sum(there.astype(jnp.int32) for there in goes)
 
-    barrier = pltpu.get_barrier_semaphore()
-    for way, there in zip(WAYS, goes):
-        @pl.when(there)
-        def _():
-            pl.semaphore_signal(barrier, inc=1, device_id=target(way), device_id_type=MESH)
-
     u_face, xf, top_face = pl.ds(0, 4), pl.ds(4, 2), pl.ds(6, 4)
     loads = [
         pltpu.make_async_copy(u_in, bar.at[0], load_sem.at[0]),
@@ -71,7 +65,14 @@
         pltpu.make_async_copy(u_in, u_out, load_sem.at[10]),
         pltpu.make_async_copy(v_in, v_out, load_sem.at[11]),
     ]
-    for load in loads:
+    for load in loads[:8]:
+        load.start()
+    barrier = pltpu.get_barrier_semaphore()
+    for way, there in zip(WAYS, goes):
+        @pl.when(there)
+        def _():
+            pl.semaphore_signal(barrier, inc=1, device_id=target(way), device_id_type=MESH)
+    for load in loads[8:]:
         load.start()
 
     def clear(there, *refs):
@@ -201,15 +202,17 @@
 
     exchanges = []
     for s in range(ITERS):
+        z_up_part = pl.ds(1, 3) if s == 0 else pl.ds(0, 4)
+        z_down_part = pl.ds(0, 1) if s == 0 else pl.ds(0, 4)
         ends = (
-            (bar.at[:, zs - 1], z_lo.at[s]),
-            (bar.at[:, 0], z_hi.at[s]),
+            (bar.at[z_up_part, zs - 1], z_lo.at[s, z_up_part]),
+            (bar.at[z_down_part, 0], z_hi.at[s, z_down_part]),
             (face.at[xf], x_lo.at[s]),
             (face.at[xf], x_hi.at[s]),
             (face.at[top_face], y_lo.at[s]),
             (face.at[u_face], y_hi.at[s]),
-            (face.at[pl.ds(0, 6)], d_a.at[s]),
-            (face.at[pl.ds(4, 6)], d_b.at[s]),
+            (face.at[xf, pl.ds(0, 1)], d_a.at[s, :, pl.ds(0, 1)]),
+            (face.at[xf, pl.ds(7, 1)], d_b.at[s, :, pl.ds(7, 1)]),
             (face.at[xf], d_c.at[s]),
             (face.at[xf], d_d.at[s]),
             (face.at[top_face, pl.ds(0, 1)], d_e.at[s, :, pl.ds(0, 1)]),
@@ -222,8 +225,8 @@
     duals = [
         (message(src, dst, way, first_send.at[k], first_recv.at[k]), goes[way], comes[way])
         for k, (src, dst, way) in enumerate((
-            (p_in.at[:, zs - 1], zp, Z_UP),
-            (q_in.at[:, 0], zq, Z_DOWN),
+            (p_out.at[:, zs - 1], zp, Z_UP),
+            (q_out.at[:, 0], zq, Z_DOWN),
             (p_in.at[:, :, ys - 1], yp, Y_UP),
             (q_in.at[:, :, 0], yq, Y_DOWN),
             (xs_own, xp, X_UP),
@@ -286,20 +289,23 @@
         cv[1] = turn_lanes(x_lo[s, 1], half_lanes)
         cv[2] = x_lo[s, 1]
 
-    def dual(z, s):
+    def dual(z, s, for_p=True, for_q=True):
         later = []
         for b in range(blocks):
             r = rows(b)
             by = half_lanes - 2 * (z * blocks + b)
-            from_x = [turn_lanes(cv[k], by) for k in range(3)]
-            t = [p_out[k, z, r, :] for k in range(3)]
-            t[0] = t[0] + SIGMA * jnp.where(last_lane, from_x[0], 0.0)
-            if b == blocks - 1:
-                t[1] = t[1] + SIGMA * jnp.where(last_row, y_hi[s, 0, pl.ds(z, 1), :], 0.0)
-            if isinstance(z, int) and z == zs - 1:
-                t[2] = t[2] + SIGMA * z_hi[s, 0, r, :]
-            for k, new in enumerate(shrink_p(t)):
-                later.append((p_out, (k, z, r), new))
+            from_x = [turn_lanes(cv[k], by) for k in range(3 if for_q else 1)]
+            if for_p:
+                t = [p_out[k, z, r, :] for k in range(3)]
+                t[0] = t[0] + SIGMA * jnp.where(last_lane, from_x[0], 0.0)
+                if b == blocks - 1:
+                    t[1] = t[1] + SIGMA * jnp.where(last_row, y_hi[s, 0, pl.ds(z, 1), :], 0.0)
+                if isinstance(z, int) and z == zs - 1:
+                    t[2] = t[2] + SIGMA * z_hi[s, 0, r, :]
+                for k, new in enumerate(shrink_p(t)):
+                    later.append((p_out, (k, z, r), new))
+            if not for_q:
+                continue
             hx = [jnp.where(first_lane, part, 0.0) for part in from_x]
             q = [q_out[k, z, r, :] for k in range(6)]
             q[XX] = q[XX] - SIGMA * hx[0]
@@ -319,6 +325,15 @@
                 later.append((q_out, (k, z, r), new))
         flush(later)
 
+    def spread(row):
+        return jnp.broadcast_to(row, (8, xs))
+
+    def column(row, lane_of_first):
+        mine = lane == lane_of_first + 2 * blocks * sub
+        return jnp.sum(jnp.where(mine, spread(row), 0.0), axis=1, keepdims=True)
+
+    where = ((0, half_lanes), (1, 0), (1, half_lanes))
+
     def halo_x(s):
         own = [face[4], face[5]]
         up_yc = jnp.where(jnp.logical_and(last_row, last_block), factor(above[1]), 1.0)
@@ -329,7 +344,7 @@
         u = got0
         v = [turn_lanes(got0, half_lanes), got1, turn_lanes(got1, half_lanes)]
         moved = turn_rows(u, -1)
-        edge_y = turn_lanes(turn_rows(d_a[s, 4], -1), 2 * (blocks - 1))
+        edge_y = turn_lanes(spread(d_a[s, 0, pl.ds(0, 1), :]), 2 * (blocks - 1))
         ahead_y = jnp.where(last_row, jnp.where(last_block, edge_y, turn_lanes(moved, -2)), moved)
         ahead_z = jnp.where(
             last_z, turn_lanes(d_c[s, 0], half_lanes - 2 * blocks), turn_lanes(u, -2 * blocks)
@@ -341,12 +356,11 @@
         got0, got1 = x_hi[s, 0], x_hi[s, 1]
         v = [turn_lanes(got0, half_lanes), got1, turn_lanes(got1, half_lanes)]
         mine = [turn_lanes(own[0], half_lanes + 1), turn_lanes(own[1], 1), turn_lanes(own[1], half_lanes + 1)]
-        where = ((0, half_lanes), (1, 0), (1, half_lanes))
         dx, dy, dz = [], [], []
         for k, (h, base) in enumerate(where):
             dx.append(v[k] - mine[k])
             moved = turn_rows(v[k], 1)
-            edge_y = turn_lanes(turn_rows(d_b[s, h], 1), -base - 2 * (blocks - 1))
+            edge_y = turn_lanes(spread(d_b[s, h, pl.ds(7, 1), :]), -base - 2 * (blocks - 1))
             behind_y = jnp.where(first_row, jnp.where(first_block, edge_y, turn_lanes(moved, 2)), moved)
             dy.append(lo_yc * v[k] - behind_y)
             edge_z = turn_lanes(d_d[s, h], -base - 2 * blocks * (zs - 1))
@@ -366,13 +380,16 @@
         lo_zr = jnp.where(first_row, factor(below[2]), 1.0)
         u = y_lo[s, 0]
         slopes = (
-            turn_lanes(jnp.where(first_lane, d_b[s, 2], u), -1) - up_x * u,
+            jnp.where(last_lane, column(d_b[s, 0, pl.ds(7, 1), :], 2 * blocks - 1), turn_lanes(u, -1)) - up_x * u,
             face[0] - u,
             jnp.where(last_row, d_e[s, 0, pl.ds(0, 1), :], turn_rows(u, -1)) - up_zr * u,
         )
         p = shrink_p([yp[k] + SIGMA * (slopes[k] - y_lo[s, 1 + k]) for k in range(3)])
         v = [y_hi[s, 1 + k] for k in range(3)]
-        dx = [lo_x * v[k] - turn_lanes(jnp.where(last_lane, d_a[s, 1 + k], v[k]), 1) for k in range(3)]
+        dx = [
+            lo_x * v[k] - jnp.where(first_lane, column(d_a[s, h, pl.ds(0, 1), :], base), turn_lanes(v[k], 1))
+            for k, (h, base) in enumerate(where)
+        ]
         dy = [v[k] - face[7 + k] for k in range(3)]
         dz = [
             lo_zr * v[k] - jnp.where(first_row, d_g[s, 1 + k, pl.ds(zs - 1, 1), :], turn_rows(v[k], 1))
@@ -383,6 +400,38 @@
             yp[k] = keep(below[1], p[k])
         for k in range(6):
             yq[k] = keep(above[1], q[k])
+
+    def halo_z_first():
+        later = []
+        for b in range(blocks):
+            r = rows(b)
+            t = [zp[k, r, :] for k in range(3)]
+            edge_x = turn_lanes(d_d[0, 0], xs - 2 - 2 * (blocks * (zs - 1) + b))
+            t[0] = t[0] + SIGMA * jnp.where(last_lane, edge_x, 0.0)
+            if b == blocks - 1:
+                t[1] = t[1] + SIGMA * jnp.where(last_row, d_g[0, 0, pl.ds(zs - 1, 1), :], 0.0)
+            t[2] = t[2] + SIGMA * bar[0, 0, r, :]
+            for k, new in enumerate(shrink_p(t)):
+                later.append((zp, (k, r), keep(below[2], new)))
+
+            hx = [
+                jnp.where(first_lane, turn_lanes(d_c[0, h], -base - 2 * b), 0.0) for h, base in where
+            ]
+            hz = [bar[1 + k, zs - 1, r, :] for k in range(3)]
+            q = [zq[k, r, :] for k in range(6)]
+            q[XX] = q[XX] - SIGMA * hx[0]
+            q[ZZ] = q[ZZ] - SIGMA * hz[2]
+            q[XY] = q[XY] - half * hx[1]
+            q[XZ] = q[XZ] - half * (hx[2] + hz[0])
+            q[YZ] = q[YZ] - half * hz[1]
+            if b == 0:
+                hy = [jnp.where(first_row, d_e[0, 1 + k, pl.ds(0, 1), :], 0.0) for k in range(3)]
+                q[YY] = q[YY] - SIGMA * hy[1]
+                q[XY] = q[XY] - half * hy[0]
+                q[YZ] = q[YZ] - half * hy[2]
+            for k, new in enumerate(shrink_q(q)):
+                later.append((zq, (k, r), keep(above[2], new)))
+        flush(later)
 
     def halo_z(s):
         later = []
@@ -404,7 +453,6 @@
                 later.append((zp, (k, r), keep(below[2], p[k])))
 
             v = [z_hi[s, 1 + k, r, :] for k in range(3)]
-            where = ((0, half_lanes), (1, 0), (1, half_lanes))
             dx, dy, dz = [], [], []
             for k, (h, base) in enumerate(where):
                 edge_x = turn_lanes(d_c[s, h], -base - 2 * b)
@@ -466,29 +514,7 @@
                 pack_bar(packed, ahead, z, b)
         flush(later)
 
-    for load in loads[:2]:
-        load.wait()
-    pl.semaphore_wait(barrier, peers)
-    start(exchanges[0][:2])
-    start(duals[:4])
-    for load in loads[2:6]:
-        load.wait()
-    start(exchanges[0][4:6])
-
-    def first_faces(z, packed):
-        for b in range(blocks):
-            pack_bar(packed, [bar[k, z, rows(b), :] for k in range(4)], z, b)
-
-    packed = each(0, zs, first_faces, (empty, empty))
-    face[4] = packed[0]
-    face[5] = packed[1]
-    start(exchanges[0][2:4])
-    start(exchanges[0][6:])
-
-    for load in loads[6:8]:
-        load.wait()
-
-    def dual_faces(z, packed):
+    def pack_dual(packed, z):
         for b in range(blocks):
             for k in range(6):
                 value = q_out[k, z, rows(b), :]
@@ -496,13 +522,6 @@
                     value = jnp.where(last_lane, p_out[k, z, rows(b), :], value)
                 packed[k] = pack(packed[k], value, 0, z * blocks + b)
 
-    for k, value in enumerate(each(0, zs, dual_faces, (empty,) * 6)):
-        xs_own[k] = value
-    start(duals[4:])
-
-    for load in loads[8:]:
-        load.wait()
-
     def prepare(z, carry):
         weight = TAU * gain[z]
         inverse = 1.0 / (1.0 + weight)
@@ -510,44 +529,102 @@
         offset[z] = weight * offset[z] * inverse
         return carry
 
-    lax.fori_loop(0, zs, prepare, 0)
-
-    def two_faces(body, carry):
-        for z in (0, zs - 1):
-            body(z, carry)
+    ends, middle = (0, zs - 1), range(1, zs - 1)
+    with jax.named_scope("load_uv"):
+        for load in loads[:2]:
+            load.wait()
+    with jax.named_scope("barrier"):
+        pl.semaphore_wait(barrier, peers)
+    with jax.named_scope("send_z0"):
+        start(exchanges[0][:2])
+        start(duals[2:4])
+    with jax.named_scope("load_face"):
+        for load in loads[2:6]:
+            load.wait()
+        start(exchanges[0][4:6])
+    with jax.named_scope("pack_uv"):
+        packed = [empty, empty]
+        for z in range(zs):
+            for b in range(blocks):
+                pack_bar(packed, [bar[k, z, rows(b), :] for k in range(4)], z, b)
+        face[4] = packed[0]
+        face[5] = packed[1]
+        start(exchanges[0][6:])
+        start(exchanges[0][2:4])
+    with jax.named_scope("load_pq"):
+        for load in loads[6:8]:
+            load.wait()
+    with jax.named_scope("pack_pq"):
+        packed = [empty] * 6
+        for z in ends:
+            pack_dual(packed, z)
+        for z in ends:
+            dual_inside(z, None)
+        start(duals[:2])
+    with jax.named_scope("pack_pq_rest"):
+        for z in middle:
+            pack_dual(packed, z)
+        for k in range(6):
+            xs_own[k] = packed[k]
+        start(duals[4:])
+    with jax.named_scope("inside0"):
+        each(1, zs - 1, dual_inside, ())
+    with jax.named_scope("prepare"):
+        for load in loads[8:]:
+            load.wait()
+        lax.fori_loop(0, zs, prepare, 0)
 
     for s in range(ITERS):
         last = s == ITERS - 1
         moves = exchanges[s]
-        each(0, zs, dual_inside, ())
-        got(moves[2:6])
-        line_up(s)
-        each(1, zs - 1, lambda z, _: dual(z, s), ())
-        got(moves[6:])
+        if s > 0:
+            with jax.named_scope(f"inside{s}"):
+                each(0, zs, dual_inside, ())
+        with jax.named_scope(f"wait_xy{s}"):
+            got(moves[2:6])
+            line_up(s)
+        with jax.named_scope(f"dual_mid{s}"):
+            dual(0, s, for_q=False)
+            for z in middle:
+                dual(z, s)
+            dual(zs - 1, s, for_p=False)
+        with jax.named_scope(f"wait_diag{s}"):
+            got(moves[6:])
         if s == 0:
-            got(duals[2:])
-        halo_x(s)
-        halo_y(s)
-        sent(moves[2:])
-        packed = list(each(2, zs - 2, lambda z, packed: primal(z, packed, last), (empty, empty)))
-        got(moves[:2])
-        sent(moves[:2])
+            with jax.named_scope(f"wait_pq{s}"):
+                got(duals[2:])
+        with jax.named_scope(f"halo_xy{s}"):
+            halo_x(s)
+            halo_y(s)
+        with jax.named_scope(f"wait_sent{s}"):
+            sent(moves[2:])
+        with jax.named_scope(f"primal_mid{s}"):
+            packed = [empty, empty]
+            for z in middle:
+                primal(z, packed, last)
+        with jax.named_scope(f"wait_z{s}"):
+            got(moves[:2])
+            sent(moves[:2])
         if s == 0:
-            got(duals[:2])
-            sent(duals)
-        halo_z(s)
-        for z in (0, zs - 1):
-            dual(z, s)
-        for z in (0, zs - 1):
-            primal(z, packed, last)
+            with jax.named_scope(f"wait_zpq{s}"):
+                got(duals[:2])
+                sent(duals)
+        with jax.named_scope(f"ends{s}"):
+            if s == 0:
+                halo_z_first()
+            else:
+                halo_z(s)
+            dual(0, s, for_p=False)
+            dual(zs - 1, s, for_q=False)
+            for z in ends:
+                primal(z, packed, last)
         if not last:
-            start(exchanges[s + 1][:2])
-        for z in (1, zs - 2):
-            primal(z, packed, last)
-        if not last:
-            face[4] = packed[0]
-            face[5] = packed[1]
-            start(exchanges[s + 1][2:])
+            with jax.named_scope(f"send{s}"):
+                face[4] = packed[0]
+                face[5] = packed[1]
+                start(exchanges[s + 1][6:])
+                start(exchanges[s + 1][2:6])
+                start(exchanges[s + 1][:2])
 
 
 def copy_out(u_in, v_in, p_in, q_in, u_out, v_out, p_out, q_out, sems):
@@ -584,8 +661,8 @@
             vmem(ITERS, 2, 8, xs),
             vmem(ITERS, 4, 8, xs),
             vmem(ITERS, 4, 8, xs),
-            vmem(ITERS, 6, 8, xs),
-            vmem(ITERS, 6, 8, xs),
+            vmem(ITERS, 2, 8, xs),
+            vmem(ITERS, 2, 8, xs),
             vmem(ITERS, 2, 8, xs),
             vmem(ITERS, 2, 8, xs),
             vmem(ITERS, 4, 8, xs),

time: 22.9 us -> 21.4 us (0.934)
  Pallas kernels: 22.1 us -> 20.6 us
    pallas_call x1, Pallas kernels: 20.9 us -> 19.4 us  [per_device(): pl.pallas_call(kernel, out_shape=tuple((pltpu.VMEM(a.shape, f32) for a in...]
where the time goes in v2:
time: 21.4 us; the launch traced here: 21.3 us
  Pallas kernels  20.6 us (96%)
  between operations  0.64 us (3%)
    pallas_call x1, Pallas kernels, per_device(): pl.pallas_call(kernel, out_shape=tuple((pltpu.VMEM(a.shape, f32) for a in...  19.4 us
    pallas_call x1, Pallas kernels, per_device(): pl.pallas_call(copy_out, out_shape=tuple((jax.ShapeDtypeStruct(a.shape, f...  1.21 us

profile of v2, /device:TPU:0, one launch (start us, length us, event | category | flops | bytes accessed | tf_op | source)
XLA Modules:
  0.0 21.3 jit_solution(10957477267266035006)
XLA Ops:
  0.6 19.4 %tgv.1 = (f32[8,32,128]{2,1,0:T(8,128)S(1)}, f32[3,8,32,128]{3,2,1,0:T(8,128)S(1)}, f32[3,8,32,128]{3,2,1,0:T(8,128)S(1)}, f32[6,8,32,128]{3,2,1,0:T(8,128)S(1)}) custom-call(f32[8,32,128]{2,1,0:T(8,128)} %noisy_in.1, f32[8,32,128]{2,1,0:T(8,128)} %fid_in.1, f32[8,32,128]{2,1,0:T(8,128)} %u_in.1, f32[3,8,32,128]{3,2,1,0:T(8,128)} %v_in.1, ...), custom_call_target="tpu_custom_call" | custom-call | tf_op jit(solution)/shard_map/tgv/pallas_call | solution.py:648
  20.1 1.2 %out.1 = (f32[8,32,128]{2,1,0:T(8,128)}, f32[3,8,32,128]{3,2,1,0:T(8,128)}, f32[3,8,32,128]{3,2,1,0:T(8,128)}, f32[6,8,32,128]{3,2,1,0:T(8,128)}) custom-call(f32[8,32,128]{2,1,0:T(8,128)S(1)} %get-tuple-element.8.u_in, f32[3,8,32,128]{3,2,1,0:T(8,128)S(1)} %get-tuple-element.9.v_in, f32[3,8,32,128]{3,2,1,0:T(8,128)S(1)} %get-tuple-element.10.p_in, ...), custom_call_target="tpu_custom_call" | custom-call | tf_op jit(solution)/shard_map/out/pallas_call | solution.py:688

commit v3 on v2

--- a/solution.py
+++ b/solution.py
@@ -23,7 +23,7 @@
     u_out, v_out, p_out, q_out,
     bar, gain, offset, face,
     z_lo, z_hi, x_lo, x_hi, y_lo, y_hi, d_a, d_b, d_c, d_d, d_e, d_g,
-    zp, zq, yp, yq, xs_own, xp, xq, cv, cp,
+    zp, zq, yp, yq, xs_own, xp, xq, cv, cp, xe, part_p, part_q,
     load_sem, send_sem, recv_sem, first_send, first_recv,
 ):
     zs, ys, xs = u_in.shape
@@ -96,9 +96,7 @@
     odd = (lane & 1) == 1
     first_lane, last_lane = lane == 0, lane == xs - 1
     first_row, last_row = sub == 0, sub == 7
-    of_block = pair & (blocks - 1)
-    first_block, last_block = of_block == 0, of_block == blocks - 1
-    first_z, last_z = pair < blocks, jnp.logical_and(pair >= pairs - blocks, pair < pairs)
+    p_pair, q_pair = (lane - half_lanes) >> 1, (lane + 1 - half_lanes) >> 1
 
     def factor(flag):
         return jnp.where(flag, jnp.float32(1), jnp.float32(0))
@@ -213,8 +211,8 @@
             (face.at[u_face], y_hi.at[s]),
             (face.at[xf, pl.ds(0, 1)], d_a.at[s, :, pl.ds(0, 1)]),
             (face.at[xf, pl.ds(7, 1)], d_b.at[s, :, pl.ds(7, 1)]),
-            (face.at[xf], d_c.at[s]),
-            (face.at[xf], d_d.at[s]),
+            (xe, d_c.at[s]),
+            (xe, d_d.at[s]),
             (face.at[top_face, pl.ds(0, 1)], d_e.at[s, :, pl.ds(0, 1)]),
             (face.at[u_face, pl.ds(zs - 1, 1)], d_g.at[s, :, pl.ds(zs - 1, 1)]),
         )
@@ -289,40 +287,60 @@
         cv[1] = turn_lanes(x_lo[s, 1], half_lanes)
         cv[2] = x_lo[s, 1]
 
-    def dual(z, s, for_p=True, for_q=True):
+    def less_q(q, x=None, y=None, z=None):
+        q = list(q)
+        if x is not None:
+            q[XX] = q[XX] - SIGMA * x[0]
+            q[XY] = q[XY] - half * x[1]
+            q[XZ] = q[XZ] - half * x[2]
+        if y is not None:
+            q[YY] = q[YY] - SIGMA * y[1]
+            q[XY] = q[XY] - half * y[0]
+            q[YZ] = q[YZ] - half * y[2]
+        if z is not None:
+            q[ZZ] = q[ZZ] - SIGMA * z[2]
+            q[XZ] = q[XZ] - half * z[0]
+            q[YZ] = q[YZ] - half * z[1]
+        return q
+
+    def dual(z, s):
         later = []
         for b in range(blocks):
             r = rows(b)
             by = half_lanes - 2 * (z * blocks + b)
-            from_x = [turn_lanes(cv[k], by) for k in range(3 if for_q else 1)]
-            if for_p:
-                t = [p_out[k, z, r, :] for k in range(3)]
-                t[0] = t[0] + SIGMA * jnp.where(last_lane, from_x[0], 0.0)
-                if b == blocks - 1:
-                    t[1] = t[1] + SIGMA * jnp.where(last_row, y_hi[s, 0, pl.ds(z, 1), :], 0.0)
-                if isinstance(z, int) and z == zs - 1:
-                    t[2] = t[2] + SIGMA * z_hi[s, 0, r, :]
+            from_x = [turn_lanes(cv[k], by) for k in range(3)]
+            t = [p_out[k, z, r, :] for k in range(3)]
+            t[0] = t[0] + SIGMA * jnp.where(last_lane, from_x[0], 0.0)
+            if b == blocks - 1:
+                t[1] = t[1] + SIGMA * jnp.where(last_row, y_hi[s, 0, pl.ds(z, 1), :], 0.0)
+            for k in range(3):
+                if z == zs - 1:
+                    later.append((part_p, (k, r), t[k]))
+            if z < zs - 1:
                 for k, new in enumerate(shrink_p(t)):
                     later.append((p_out, (k, z, r), new))
-            if not for_q:
-                continue
             hx = [jnp.where(first_lane, part, 0.0) for part in from_x]
-            q = [q_out[k, z, r, :] for k in range(6)]
-            q[XX] = q[XX] - SIGMA * hx[0]
-            q[XY] = q[XY] - half * hx[1]
-            q[XZ] = q[XZ] - half * hx[2]
+            hy = None
             if b == 0:
                 hy = [jnp.where(first_row, y_lo[s, 1 + k, pl.ds(z, 1), :], 0.0) for k in range(3)]
-                q[YY] = q[YY] - SIGMA * hy[1]
-                q[XY] = q[XY] - half * hy[0]
-                q[YZ] = q[YZ] - half * hy[2]
-            if isinstance(z, int) and z == 0:
-                hz = [z_lo[s, 1 + k, r, :] for k in range(3)]
-                q[ZZ] = q[ZZ] - SIGMA * hz[2]
-                q[XZ] = q[XZ] - half * hz[0]
-                q[YZ] = q[YZ] - half * hz[1]
+            q = less_q([q_out[k, z, r, :] for k in range(6)], hx, hy)
+            if z > 0:
+                q = shrink_q(q)
+            for k in range(6):
+                later.append((part_q, (k, r), q[k]) if z == 0 else (q_out, (k, z, r), q[k]))
+        flush(later)
+
+    def dual_ends(s):
+        later = []
+        for b in range(blocks):
+            r = rows(b)
+            t = [part_p[k, r, :] for k in range(3)]
+            t[2] = t[2] + SIGMA * z_hi[s, 0, r, :]
+            for k, new in enumerate(shrink_p(t)):
+                later.append((p_out, (k, zs - 1, r), new))
+            q = less_q([part_q[k, r, :] for k in range(6)], z=[z_lo[s, 1 + k, r, :] for k in range(3)])
             for k, new in enumerate(shrink_q(q)):
-                later.append((q_out, (k, z, r), new))
+                later.append((q_out, (k, 0, r), new))
         flush(later)
 
     def spread(row):
@@ -334,68 +352,91 @@
 
     where = ((0, half_lanes), (1, 0), (1, half_lanes))
 
-    def halo_x(s):
-        own = [face[4], face[5]]
-        up_yc = jnp.where(jnp.logical_and(last_row, last_block), factor(above[1]), 1.0)
-        lo_yc = jnp.where(jnp.logical_and(first_row, first_block), factor(below[1]), 1.0)
-        up_zc = jnp.where(last_z, factor(above[2]), 1.0)
-        lo_zc = jnp.where(first_z, factor(below[2]), 1.0)
-        got0, got1 = x_lo[s, 0], x_lo[s, 1]
-        u = got0
-        v = [turn_lanes(got0, half_lanes), got1, turn_lanes(got1, half_lanes)]
+    def halo_x_inside(s):
+        far = pairs - blocks
+        up_yc = jnp.where(jnp.logical_and(last_row, (p_pair & (blocks - 1)) == blocks - 1), factor(above[1]), 1.0)
+        lo_yc = jnp.where(jnp.logical_and(first_row, (q_pair & (blocks - 1)) == 0), factor(below[1]), 1.0)
+        up_zc = jnp.where(p_pair >= far, factor(above[2]), 1.0)
+        lo_zc = jnp.where(q_pair < blocks, factor(below[2]), 1.0)
+        u = turn_lanes(x_lo[s, 0], half_lanes)
+        v = [x_lo[s, 0], turn_lanes(x_lo[s, 1], half_lanes), x_lo[s, 1]]
+        own = turn_lanes(face[4], half_lanes - 1)
         moved = turn_rows(u, -1)
-        edge_y = turn_lanes(spread(d_a[s, 0, pl.ds(0, 1), :]), 2 * (blocks - 1))
-        ahead_y = jnp.where(last_row, jnp.where(last_block, edge_y, turn_lanes(moved, -2)), moved)
-        ahead_z = jnp.where(
-            last_z, turn_lanes(d_c[s, 0], half_lanes - 2 * blocks), turn_lanes(u, -2 * blocks)
-        )
-        slopes = (turn_lanes(own[0], -1) - u, ahead_y - up_yc * u, ahead_z - up_zc * u)
-        p = shrink_p([xp[k] + SIGMA * (slopes[k] - v[k]) for k in range(3)])
-        p = [keep(below[0], part) for part in p]
-
-        got0, got1 = x_hi[s, 0], x_hi[s, 1]
-        v = [turn_lanes(got0, half_lanes), got1, turn_lanes(got1, half_lanes)]
-        mine = [turn_lanes(own[0], half_lanes + 1), turn_lanes(own[1], 1), turn_lanes(own[1], half_lanes + 1)]
+        turned = jnp.where((p_pair & (blocks - 1)) == blocks - 1, 0.0, turn_lanes(moved, -2))
+        ahead_y = jnp.where(last_row, turned, moved)
+        ahead_z = jnp.where(p_pair >= far, 0.0, turn_lanes(u, -2 * blocks))
+        slopes = (own - u, ahead_y - up_yc * u, ahead_z - up_zc * u)
+        for k in range(3):
+            xp[k] = xp[k] + SIGMA * (slopes[k] - v[k])
+
+        v = [turn_lanes(x_hi[s, 0], -2), turn_lanes(x_hi[s, 1], half_lanes - 2), turn_lanes(x_hi[s, 1], -2)]
+        mine = [turn_lanes(face[4], -1), turn_lanes(face[5], half_lanes - 1), turn_lanes(face[5], -1)]
         dx, dy, dz = [], [], []
-        for k, (h, base) in enumerate(where):
+        for k in range(3):
             dx.append(v[k] - mine[k])
             moved = turn_rows(v[k], 1)
-            edge_y = turn_lanes(spread(d_b[s, h, pl.ds(7, 1), :]), -base - 2 * (blocks - 1))
-            behind_y = jnp.where(first_row, jnp.where(first_block, edge_y, turn_lanes(moved, 2)), moved)
-            dy.append(lo_yc * v[k] - behind_y)
-            edge_z = turn_lanes(d_d[s, h], -base - 2 * blocks * (zs - 1))
-            dz.append(lo_zc * v[k] - jnp.where(first_z, edge_z, turn_lanes(v[k], 2 * blocks)))
-        q = shrink_q(grow_q([xq[k] for k in range(6)], dx, dy, dz))
+            turned = jnp.where((q_pair & (blocks - 1)) == 0, 0.0, turn_lanes(moved, 2))
+            dy.append(lo_yc * v[k] - jnp.where(first_row, turned, moved))
+            dz.append(lo_zc * v[k] - jnp.where(q_pair < blocks, 0.0, turn_lanes(v[k], 2 * blocks)))
+        q = [turn_lanes(xq[k], -2) if s == 0 else xq[k] for k in range(6)]
+        for k, new in enumerate(grow_q(q, dx, dy, dz)):
+            xq[k] = new
+
+    def halo_x(s):
+        far = pairs - blocks
+        t = [xp[k] for k in range(3)]
+        edge = turn_lanes(spread(d_a[s, 0, pl.ds(0, 1), :]), half_lanes + 2 * (blocks - 1))
+        here = jnp.logical_and(last_row, (p_pair & (blocks - 1)) == blocks - 1)
+        t[1] = t[1] + SIGMA * jnp.where(here, edge, 0.0)
+        edge = turn_lanes(d_c[s, 0], half_lanes + 2 * far)
+        t[2] = t[2] + SIGMA * jnp.where(p_pair >= far, edge, 0.0)
+        p = [keep(below[0], part) for part in shrink_p(t)]
+        here = jnp.logical_and(first_row, (q_pair & (blocks - 1)) == 0)
+        edge_y, edge_z = [], []
+        for h, base in where:
+            edge = turn_lanes(spread(d_b[s, h, pl.ds(7, 1), :]), half_lanes - 2 * blocks - base)
+            edge_y.append(jnp.where(here, edge, 0.0))
+            edge = turn_lanes(d_d[s, h], half_lanes - 2 - 2 * far - base)
+            edge_z.append(jnp.where(q_pair < blocks, edge, 0.0))
+        q = shrink_q(less_q([xq[k] for k in range(6)], y=edge_y, z=edge_z))
         q = [keep(above[0], part) for part in q]
         for k in range(3):
             xp[k] = p[k]
         for k in range(6):
             xq[k] = q[k]
-        cp[0] = jnp.where(odd, turn_lanes(q[XX], half_lanes - 2), turn_lanes(p[0], half_lanes))
-        cp[1] = turn_lanes(q[XY], half_lanes - 2)
-        cp[2] = turn_lanes(q[XZ], half_lanes - 2)
-
-    def halo_y(s):
+        cp[0] = jnp.where(odd, q[XX], p[0])
+        cp[1] = q[XY]
+        cp[2] = q[XZ]
+
+    def halo_y_inside(s):
         up_zr = jnp.where(last_row, factor(above[2]), 1.0)
         lo_zr = jnp.where(first_row, factor(below[2]), 1.0)
         u = y_lo[s, 0]
         slopes = (
-            jnp.where(last_lane, column(d_b[s, 0, pl.ds(7, 1), :], 2 * blocks - 1), turn_lanes(u, -1)) - up_x * u,
+            next_x(u) - up_x * u,
             face[0] - u,
-            jnp.where(last_row, d_e[s, 0, pl.ds(0, 1), :], turn_rows(u, -1)) - up_zr * u,
+            jnp.where(last_row, 0.0, turn_rows(u, -1)) - up_zr * u,
         )
-        p = shrink_p([yp[k] + SIGMA * (slopes[k] - y_lo[s, 1 + k]) for k in range(3)])
+        for k in range(3):
+            yp[k] = yp[k] + SIGMA * (slopes[k] - y_lo[s, 1 + k])
         v = [y_hi[s, 1 + k] for k in range(3)]
-        dx = [
-            lo_x * v[k] - jnp.where(first_lane, column(d_a[s, h, pl.ds(0, 1), :], base), turn_lanes(v[k], 1))
-            for k, (h, base) in enumerate(where)
+        dx = [lo_x * v[k] - prev_x(v[k]) for k in range(3)]
+        dy = [v[k] - face[7 + k] for k in range(3)]
+        dz = [lo_zr * v[k] - jnp.where(first_row, 0.0, turn_rows(v[k], 1)) for k in range(3)]
+        for k, new in enumerate(grow_q([yq[k] for k in range(6)], dx, dy, dz)):
+            yq[k] = new
+
+    def halo_y(s):
+        t = [yp[k] for k in range(3)]
+        edge = column(d_b[s, 0, pl.ds(7, 1), :], 2 * blocks - 1)
+        t[0] = t[0] + SIGMA * jnp.where(last_lane, edge, 0.0)
+        t[2] = t[2] + SIGMA * jnp.where(last_row, d_e[s, 0, pl.ds(0, 1), :], 0.0)
+        p = shrink_p(t)
+        edge_x = [
+            jnp.where(first_lane, column(d_a[s, h, pl.ds(0, 1), :], base), 0.0) for h, base in where
         ]
-        dy = [v[k] - face[7 + k] for k in range(3)]
-        dz = [
-            lo_zr * v[k] - jnp.where(first_row, d_g[s, 1 + k, pl.ds(zs - 1, 1), :], turn_rows(v[k], 1))
-            for k in range(3)
-        ]
-        q = shrink_q(grow_q([yq[k] for k in range(6)], dx, dy, dz))
+        edge_z = [jnp.where(first_row, d_g[s, 1 + k, pl.ds(zs - 1, 1), :], 0.0) for k in range(3)]
+        q = shrink_q(less_q([yq[k] for k in range(6)], x=edge_x, z=edge_z))
         for k in range(3):
             yp[k] = keep(below[1], p[k])
         for k in range(6):
@@ -418,17 +459,10 @@
                 jnp.where(first_lane, turn_lanes(d_c[0, h], -base - 2 * b), 0.0) for h, base in where
             ]
             hz = [bar[1 + k, zs - 1, r, :] for k in range(3)]
-            q = [zq[k, r, :] for k in range(6)]
-            q[XX] = q[XX] - SIGMA * hx[0]
-            q[ZZ] = q[ZZ] - SIGMA * hz[2]
-            q[XY] = q[XY] - half * hx[1]
-            q[XZ] = q[XZ] - half * (hx[2] + hz[0])
-            q[YZ] = q[YZ] - half * hz[1]
+            hy = None
             if b == 0:
                 hy = [jnp.where(first_row, d_e[0, 1 + k, pl.ds(0, 1), :], 0.0) for k in range(3)]
-                q[YY] = q[YY] - SIGMA * hy[1]
-                q[XY] = q[XY] - half * hy[0]
-                q[YZ] = q[YZ] - half * hy[2]
+            q = less_q([zq[k, r, :] for k in range(6)], hx, hy, hz)
             for k, new in enumerate(shrink_q(q)):
                 later.append((zq, (k, r), keep(above[2], new)))
         flush(later)
@@ -468,7 +502,11 @@
                 later.append((zq, (k, r), keep(above[2], q[k])))
         flush(later)
 
-    def primal(z, packed, last):
+    def pack_plane(packed, z):
+        for b in range(blocks):
+            pack_bar(packed, [bar[k, z, rows(b), :] for k in range(4)], z, b)
+
+    def primal(z, last):
         later = []
         z_up, z_lo_ = up_z(z), lo_z(z)
         at_start = isinstance(z, int) and z == 0
@@ -511,7 +549,6 @@
                         later.append((face, (k, pl.ds(z, 1)), ahead[k][0:1, :]))
                     if b == blocks - 1:
                         later.append((face, (6 + k, pl.ds(z, 1)), ahead[k][7:8, :]))
-                pack_bar(packed, ahead, z, b)
         flush(later)
 
     def pack_dual(packed, z):
@@ -520,7 +557,7 @@
                 value = q_out[k, z, rows(b), :]
                 if k < 3:
                     value = jnp.where(last_lane, p_out[k, z, rows(b), :], value)
-                packed[k] = pack(packed[k], value, 0, z * blocks + b)
+                packed[k] = pack(packed[k], value, pairs, z * blocks + b)
 
     def prepare(z, carry):
         weight = TAU * gain[z]
@@ -544,12 +581,16 @@
         start(exchanges[0][4:6])
     with jax.named_scope("pack_uv"):
         packed = [empty, empty]
-        for z in range(zs):
-            for b in range(blocks):
-                pack_bar(packed, [bar[k, z, rows(b), :] for k in range(4)], z, b)
+        for z in ends:
+            pack_plane(packed, z)
+        xe[0] = packed[0]
+        xe[1] = packed[1]
+        for z in middle:
+            pack_plane(packed, z)
         face[4] = packed[0]
         face[5] = packed[1]
-        start(exchanges[0][6:])
+        start(exchanges[0][8:])
+        start(exchanges[0][6:8])
         start(exchanges[0][2:4])
     with jax.named_scope("load_pq"):
         for load in loads[6:8]:
@@ -584,27 +625,24 @@
             got(moves[2:6])
             line_up(s)
         with jax.named_scope(f"dual_mid{s}"):
-            dual(0, s, for_q=False)
-            for z in middle:
+            for z in range(zs):
                 dual(z, s)
-            dual(zs - 1, s, for_p=False)
-        with jax.named_scope(f"wait_diag{s}"):
-            got(moves[6:])
+            if s > 0:
+                halo_x_inside(s)
+                halo_y_inside(s)
         if s == 0:
             with jax.named_scope(f"wait_pq{s}"):
                 got(duals[2:])
+                halo_x_inside(s)
+                halo_y_inside(s)
+        with jax.named_scope(f"wait_diag{s}"):
+            got(moves[6:])
         with jax.named_scope(f"halo_xy{s}"):
             halo_x(s)
             halo_y(s)
-        with jax.named_scope(f"wait_sent{s}"):
-            sent(moves[2:])
-        with jax.named_scope(f"primal_mid{s}"):
-            packed = [empty, empty]
-            for z in middle:
-                primal(z, packed, last)
         with jax.named_scope(f"wait_z{s}"):
             got(moves[:2])
-            sent(moves[:2])
+            sent(moves)
         if s == 0:
             with jax.named_scope(f"wait_zpq{s}"):
                 got(duals[:2])
@@ -614,17 +652,31 @@
                 halo_z_first()
             else:
                 halo_z(s)
-            dual(0, s, for_p=False)
-            dual(zs - 1, s, for_q=False)
+            dual_ends(s)
             for z in ends:
-                primal(z, packed, last)
+                primal(z, last)
+            if not last:
+                packed = [empty, empty]
+                for z in ends:
+                    pack_plane(packed, z)
+                xe[0] = packed[0]
+                xe[1] = packed[1]
+        if not last:
+            with jax.named_scope(f"send_z{s}"):
+                start(exchanges[s + 1][8:])
+                start(exchanges[s + 1][:2])
+        with jax.named_scope(f"primal_mid{s}"):
+            for z in middle:
+                primal(z, last)
+            if not last:
+                for z in middle:
+                    pack_plane(packed, z)
+                face[4] = packed[0]
+                face[5] = packed[1]
         if not last:
             with jax.named_scope(f"send{s}"):
-                face[4] = packed[0]
-                face[5] = packed[1]
-                start(exchanges[s + 1][6:])
+                start(exchanges[s + 1][6:8])
                 start(exchanges[s + 1][2:6])
-                start(exchanges[s + 1][:2])
 
 
 def copy_out(u_in, v_in, p_in, q_in, u_out, v_out, p_out, q_out, sems):
@@ -676,6 +728,9 @@
             vmem(6, 8, xs),
             vmem(3, 8, xs),
             vmem(3, 8, xs),
+            vmem(2, 8, xs),
+            vmem(3, ys, xs),
+            vmem(6, ys, xs),
             pltpu.SemaphoreType.DMA((12,)),
             pltpu.SemaphoreType.DMA((ITERS, 12)),
             pltpu.SemaphoreType.DMA((ITERS, 12)),

time: 21.4 us -> 20.5 us (0.958)
  Pallas kernels: 20.6 us -> 19.7 us
    pallas_call x1, Pallas kernels: 19.4 us -> 18.5 us  [per_device(): pl.pallas_call(kernel, out_shape=tuple((pltpu.VMEM(a.shape, f32) for a in...]
where the time goes in v3:
time: 20.5 us; the launch traced here: 20.3 us
  Pallas kernels  19.7 us (96%)
  between operations  0.64 us (3%)
    pallas_call x1, Pallas kernels, per_device(): pl.pallas_call(kernel, out_shape=tuple((pltpu.VMEM(a.shape, f32) for a in...  18.5 us
    pallas_call x1, Pallas kernels, per_device(): pl.pallas_call(copy_out, out_shape=tuple((jax.ShapeDtypeStruct(a.shape, f...  1.21 us

profile of v3, /device:TPU:0, one launch (start us, length us, event | category | flops | bytes accessed | tf_op | source)
XLA Modules:
  0.0 20.3 jit_solution(8539965691758001910)
XLA Ops:
  0.6 18.5 %tgv.1 = (f32[8,32,128]{2,1,0:T(8,128)S(1)}, f32[3,8,32,128]{3,2,1,0:T(8,128)S(1)}, f32[3,8,32,128]{3,2,1,0:T(8,128)S(1)}, f32[6,8,32,128]{3,2,1,0:T(8,128)S(1)}) custom-call(f32[8,32,128]{2,1,0:T(8,128)} %noisy_in.1, f32[8,32,128]{2,1,0:T(8,128)} %fid_in.1, f32[8,32,128]{2,1,0:T(8,128)} %u_in.1, f32[3,8,32,128]{3,2,1,0:T(8,128)} %v_in.1, ...), custom_call_target="tpu_custom_call" | custom-call | tf_op jit(solution)/shard_map/tgv/pallas_call | solution.py:700
  19.1 1.2 %out.1 = (f32[8,32,128]{2,1,0:T(8,128)}, f32[3,8,32,128]{3,2,1,0:T(8,128)}, f32[3,8,32,128]{3,2,1,0:T(8,128)}, f32[6,8,32,128]{3,2,1,0:T(8,128)}) custom-call(f32[8,32,128]{2,1,0:T(8,128)S(1)} %get-tuple-element.8.u_in, f32[3,8,32,128]{3,2,1,0:T(8,128)S(1)} %get-tuple-element.9.v_in, f32[3,8,32,128]{3,2,1,0:T(8,128)S(1)} %get-tuple-element.10.p_in, ...), custom_call_target="tpu_custom_call" | custom-call | tf_op jit(solution)/shard_map/out/pallas_call | solution.py:743

commit v4 on v3

--- a/solution.py
+++ b/solution.py
@@ -10,6 +10,7 @@
 ALPHA1, ALPHA0, SIGMA, TAU = 0.5, 1.0, 0.2, 0.2
 XX, YY, ZZ, XY, XZ, YZ = range(6)
 PARTS = ((XX, XY, XZ), (XY, YY, YZ), (XZ, YZ, ZZ))
+Y_PARTS, Z_PARTS = (XY, YY, YZ), (XZ, YZ, ZZ)
 MESH = pl.DeviceIdType.MESH
 Z_UP, Z_DOWN, X_UP, X_DOWN, Y_UP, Y_DOWN, XY_A, XY_B, XZ_A, XZ_B, YZ_A, YZ_B = range(12)
 WAYS = (
@@ -18,12 +19,58 @@
 )
 
 
+def primal_plane(z, below, above, u_ref, v_ref, p_ref, q_ref, gain, offset, halo):
+    zs, ys, xs = u_ref.shape
+    blocks = ys // 8
+    cp, row_p, row_q, plane_p, plane_q = halo
+    lane = lax.broadcasted_iota(jnp.int32, (8, xs), 1)
+    sub = lax.broadcasted_iota(jnp.int32, (8, xs), 0)
+    first_lane, last_lane = lane == 0, lane == xs - 1
+    first_row, last_row = sub == 0, sub == 7
+
+    def factor(flag):
+        return jnp.where(flag, jnp.float32(1), jnp.float32(0))
+
+    up_x = jnp.where(last_lane, factor(above[0]), 1.0)
+    lo_x = jnp.where(first_lane, factor(below[0]), 1.0)
+    up_z = factor(above[2]) if z == zs - 1 else 1.0
+    lo_z = factor(below[2]) if z == 0 else 1.0
+    for b in range(blocks):
+        r = pl.ds(8 * b, 8)
+        up_y = jnp.where(last_row, factor(above[1]), 1.0) if b == blocks - 1 else 1.0
+        lo_y = jnp.where(first_row, factor(below[1]), 1.0) if b == 0 else 1.0
+        by = xs // 2 - 2 * (z * blocks + b)
+        from_x = [pltpu.roll(cp[k], by, 1) for k in range(3)]
+        p = [p_ref[k, z, r, :] for k in range(3)]
+        q = [q_ref[k, z, r, :] for k in range(6)]
+        before_x = jnp.where(first_lane, from_x[0], pltpu.roll(p[0], 1, 1))
+        if b > 0:
+            before_y = p_ref[1, z, pl.ds(8 * b - 1, 8), :]
+        else:
+            before_y = jnp.where(first_row, row_p(z), pltpu.roll(p[1], 1, 0))
+        before_z = plane_p(r) if z == 0 else p_ref[2, z - 1, r, :]
+        div = (up_x * p[0] - before_x) + (up_y * p[1] - before_y) + (up_z * p[2] - before_z)
+        old = u_ref[z, r, :]
+        pieces = [((old + TAU * div) * gain[z, r, :] + offset[z, r, :], old)]
+        for k, (ax, ay, az) in enumerate(PARTS):
+            after_x = jnp.where(last_lane, from_x[k], pltpu.roll(q[ax], xs - 1, 1))
+            if b < blocks - 1:
+                after_y = q_ref[ay, z, pl.ds(8 * b + 1, 8), :]
+            else:
+                after_y = jnp.where(last_row, row_q(ay, z), pltpu.roll(q[ay], 7, 0))
+            after_z = plane_q(az, r) if z == zs - 1 else q_ref[az, z + 1, r, :]
+            div2 = (after_x - lo_x * q[ax]) + (after_y - lo_y * q[ay]) + (after_z - lo_z * q[az])
+            old = v_ref[k, z, r, :]
+            pieces.append((old + TAU * (p[k] + div2), old))
+        yield b, r, pieces
+
+
 def kernel(
     noisy_in, fid_in, u_in, v_in, p_in, q_in,
-    u_out, v_out, p_out, q_out,
-    bar, gain, offset, face,
+    u_out, v_out, p_out, q_out, gain, offset, cp, edge_y, edge_z,
+    bar, face,
     z_lo, z_hi, x_lo, x_hi, y_lo, y_hi, d_a, d_b, d_c, d_d, d_e, d_g,
-    zp, zq, yp, yq, xs_own, xp, xq, cv, cp, xe, part_p, part_q,
+    zp, zq, yp, yq, xs_own, xp, xq, cv, xe, part_p, part_q,
     load_sem, send_sem, recv_sem, first_send, first_recv,
 ):
     zs, ys, xs = u_in.shape
@@ -58,21 +105,23 @@
         pltpu.make_async_copy(v_in.at[:, :, 0], face.at[pl.ds(1, 3)], load_sem.at[3]),
         pltpu.make_async_copy(u_in.at[:, ys - 1], face.at[6], load_sem.at[4]),
         pltpu.make_async_copy(v_in.at[:, :, ys - 1], face.at[pl.ds(7, 3)], load_sem.at[5]),
-        pltpu.make_async_copy(p_in, p_out, load_sem.at[6]),
-        pltpu.make_async_copy(q_in, q_out, load_sem.at[7]),
+        pltpu.make_async_copy(q_in, q_out, load_sem.at[6]),
+        pltpu.make_async_copy(p_in, p_out, load_sem.at[7]),
         pltpu.make_async_copy(noisy_in, offset, load_sem.at[8]),
         pltpu.make_async_copy(fid_in, gain, load_sem.at[9]),
         pltpu.make_async_copy(u_in, u_out, load_sem.at[10]),
         pltpu.make_async_copy(v_in, v_out, load_sem.at[11]),
     ]
-    for load in loads[:8]:
+    for load in loads[:2]:
         load.start()
+
     barrier = pltpu.get_barrier_semaphore()
     for way, there in zip(WAYS, goes):
         @pl.when(there)
         def _():
             pl.semaphore_signal(barrier, inc=1, device_id=target(way), device_id_type=MESH)
-    for load in loads[8:]:
+
+    for load in loads[2:8]:
         load.start()
 
     def clear(there, *refs):
@@ -506,49 +555,25 @@
         for b in range(blocks):
             pack_bar(packed, [bar[k, z, rows(b), :] for k in range(4)], z, b)
 
-    def primal(z, last):
+    halo = (
+        cp,
+        lambda z: yp[1, pl.ds(z, 1), :],
+        lambda k, z: yq[k, pl.ds(z, 1), :],
+        lambda r: zp[2, r, :],
+        lambda k, r: zq[k, r, :],
+    )
+
+    def primal(z):
         later = []
-        z_up, z_lo_ = up_z(z), lo_z(z)
-        at_start = isinstance(z, int) and z == 0
-        at_end = isinstance(z, int) and z == zs - 1
-        for b in range(blocks):
-            r = rows(b)
-            by = half_lanes - 2 * (z * blocks + b)
-            from_x = [turn_lanes(cp[k], by) for k in range(3)]
-            p = [p_out[k, z, r, :] for k in range(3)]
-            before_x = jnp.where(first_lane, from_x[0], pltpu.roll(p[0], 1, 1))
-            if b > 0:
-                before_y = p_out[1, z, rows(b, -1), :]
-            else:
-                before_y = jnp.where(first_row, yp[1, pl.ds(z, 1), :], pltpu.roll(p[1], 1, 0))
-            before_z = zp[2, r, :] if at_start else p_out[2, z - 1, r, :]
-            div = (up_x * p[0] - before_x) + (up_y(b, p[1]) - before_y) + (z_up * p[2] - before_z)
-            old = u_out[z, r, :]
-            new = (old + TAU * div) * gain[z, r, :] + offset[z, r, :]
-            later.append((u_out, (z, r), new))
-            ahead = [2.0 * new - old]
-            q = [q_out[k, z, r, :] for k in range(6)]
-            for k, (ax, ay, az) in enumerate(PARTS):
-                after_x = jnp.where(last_lane, from_x[k], pltpu.roll(q[ax], xs - 1, 1))
-                if b < blocks - 1:
-                    after_y = q_out[ay, z, rows(b, 1), :]
-                else:
-                    after_y = jnp.where(last_row, yq[ay, pl.ds(z, 1), :], pltpu.roll(q[ay], 7, 0))
-                after_z = zq[az, r, :] if at_end else q_out[az, z + 1, r, :]
-                div2 = (
-                    (after_x - lo_x * q[ax]) + (after_y - lo_y(b, q[ay])) + (after_z - z_lo_ * q[az])
-                )
-                old = v_out[k, z, r, :]
-                new = old + TAU * (p[k] + div2)
-                later.append((v_out, (k, z, r), new))
-                ahead.append(2.0 * new - old)
-            if not last:
-                for k in range(4):
-                    later.append((bar, (k, z, r), ahead[k]))
-                    if b == 0:
-                        later.append((face, (k, pl.ds(z, 1)), ahead[k][0:1, :]))
-                    if b == blocks - 1:
-                        later.append((face, (6 + k, pl.ds(z, 1)), ahead[k][7:8, :]))
+        for b, r, pieces in primal_plane(z, below, above, u_out, v_out, p_out, q_out, gain, offset, halo):
+            for k, (new, old) in enumerate(pieces):
+                later.append((u_out, (z, r), new) if k == 0 else (v_out, (k - 1, z, r), new))
+                ahead = 2.0 * new - old
+                later.append((bar, (k, z, r), ahead))
+                if b == 0:
+                    later.append((face, (k, pl.ds(z, 1)), ahead[0:1, :]))
+                if b == blocks - 1:
+                    later.append((face, (6 + k, pl.ds(z, 1)), ahead[7:8, :]))
         flush(later)
 
     def pack_dual(packed, z):
@@ -575,6 +600,8 @@
     with jax.named_scope("send_z0"):
         start(exchanges[0][:2])
         start(duals[2:4])
+        for load in loads[8:]:
+            load.start()
     with jax.named_scope("load_face"):
         for load in loads[2:6]:
             load.wait()
@@ -653,37 +680,71 @@
             else:
                 halo_z(s)
             dual_ends(s)
+            if last:
+                edge_y[0] = yp[1]
+                edge_z[0] = zp[2]
+                for at, k in enumerate(Y_PARTS):
+                    edge_y[1 + at] = yq[k]
+                for at, k in enumerate(Z_PARTS):
+                    edge_z[1 + at] = zq[k]
+                continue
+            packed = [empty, empty]
             for z in ends:
-                primal(z, last)
-            if not last:
-                packed = [empty, empty]
-                for z in ends:
-                    pack_plane(packed, z)
-                xe[0] = packed[0]
-                xe[1] = packed[1]
-        if not last:
-            with jax.named_scope(f"send_z{s}"):
-                start(exchanges[s + 1][8:])
-                start(exchanges[s + 1][:2])
+                primal(z)
+            for z in ends:
+                pack_plane(packed, z)
+            xe[0] = packed[0]
+            xe[1] = packed[1]
+        with jax.named_scope(f"send_z{s}"):
+            start(exchanges[s + 1][8:])
+            start(exchanges[s + 1][:2])
         with jax.named_scope(f"primal_mid{s}"):
             for z in middle:
-                primal(z, last)
-            if not last:
-                for z in middle:
-                    pack_plane(packed, z)
-                face[4] = packed[0]
-                face[5] = packed[1]
-        if not last:
-            with jax.named_scope(f"send{s}"):
-                start(exchanges[s + 1][6:8])
-                start(exchanges[s + 1][2:6])
-
-
-def copy_out(u_in, v_in, p_in, q_in, u_out, v_out, p_out, q_out, sems):
-    pairs = ((q_in, q_out), (p_in, p_out), (v_in, v_out), (u_in, u_out))
-    copies = [pltpu.make_async_copy(a, b, sems.at[i]) for i, (a, b) in enumerate(pairs)]
+                primal(z)
+            for z in middle:
+                pack_plane(packed, z)
+            face[4] = packed[0]
+            face[5] = packed[1]
+        with jax.named_scope(f"send{s}"):
+            start(exchanges[s + 1][6:8])
+            start(exchanges[s + 1][2:6])
+
+
+def last_primal(
+    u_in, v_in, p_in, q_in, gain, offset, cp, edge_y, edge_z,
+    u_out, v_out, p_out, q_out,
+    u_new, v_new, sems,
+):
+    zs, ys, xs = u_in.shape
+    place = [lax.axis_index(a) for a in AXES]
+    count = [lax.axis_size(a) for a in AXES]
+    below = [place[i] > 0 for i in range(3)]
+    above = [place[i] < count[i] - 1 for i in range(3)]
+    copies = [pltpu.make_async_copy(q_in.at[k], q_out.at[k], sems.at[k]) for k in range(6)]
+    copies += [pltpu.make_async_copy(p_in.at[k], p_out.at[k], sems.at[6 + k]) for k in range(3)]
     for copy in copies:
         copy.start()
+    halo = (
+        cp,
+        lambda z: edge_y[0, pl.ds(z, 1), :],
+        lambda k, z: edge_y[1 + Y_PARTS.index(k), pl.ds(z, 1), :],
+        lambda r: edge_z[0, r, :],
+        lambda k, r: edge_z[1 + Z_PARTS.index(k), r, :],
+    )
+    for z in range(zs):
+        for _, r, pieces in primal_plane(z, below, above, u_in, v_in, p_in, q_in, gain, offset, halo):
+            u_new[z, r, :] = pieces[0][0]
+            for k in range(3):
+                v_new[k, z, r, :] = pieces[1 + k][0]
+        if z % 2 == 1:
+            two = pl.ds(z - 1, 2)
+            mine = [
+                pltpu.make_async_copy(v_new.at[:, two], v_out.at[:, two], sems.at[9 + z - 1]),
+                pltpu.make_async_copy(u_new.at[two], u_out.at[two], sems.at[9 + z]),
+            ]
+            for copy in mine:
+                copy.start()
+            copies += mine
     for copy in copies:
         copy.wait()
 
@@ -697,15 +758,15 @@
     def vmem(*shape):
         return pltpu.VMEM(shape, f32)
 
+    shapes = [a.shape for a in (primal_u, primal_v, dual_p, dual_q)]
+    kept = shapes + [(zs, ys, xs), (zs, ys, xs), (3, 8, xs), (4, 8, xs), (4, ys, xs)]
     results = pl.pallas_call(
         kernel,
-        out_shape=tuple(pltpu.VMEM(a.shape, f32) for a in (primal_u, primal_v, dual_p, dual_q)),
+        out_shape=tuple(vmem(*shape) for shape in kept),
         in_specs=[pl.BlockSpec(memory_space=pl.ANY)] * 6,
-        out_specs=tuple([pl.BlockSpec(memory_space=pltpu.VMEM)] * 4),
+        out_specs=tuple([pl.BlockSpec(memory_space=pltpu.VMEM)] * len(kept)),
         scratch_shapes=[
             vmem(4, zs, ys, xs),
-            vmem(zs, ys, xs),
-            vmem(zs, ys, xs),
             vmem(10, 8, xs),
             vmem(ITERS, 4, ys, xs),
             vmem(ITERS, 4, ys, xs),
@@ -727,7 +788,6 @@
             vmem(6, 8, xs),
             vmem(6, 8, xs),
             vmem(3, 8, xs),
-            vmem(3, 8, xs),
             vmem(2, 8, xs),
             vmem(3, ys, xs),
             vmem(6, ys, xs),
@@ -741,11 +801,15 @@
         name="tgv",
     )(noisy_image, fidelity, primal_u, primal_v, dual_p, dual_q)
     return pl.pallas_call(
-        copy_out,
-        out_shape=tuple(jax.ShapeDtypeStruct(a.shape, f32) for a in results),
-        in_specs=[pl.BlockSpec(memory_space=pltpu.VMEM)] * 4,
+        last_primal,
+        out_shape=tuple(jax.ShapeDtypeStruct(shape, f32) for shape in shapes),
+        in_specs=[pl.BlockSpec(memory_space=pltpu.VMEM)] * len(kept),
         out_specs=tuple([pl.BlockSpec(memory_space=pl.ANY)] * 4),
-        scratch_shapes=[pltpu.SemaphoreType.DMA((4,))],
+        scratch_shapes=[
+            vmem(zs, ys, xs),
+            vmem(3, zs, ys, xs),
+            pltpu.SemaphoreType.DMA((9 + zs,)),
+        ],
         name="out",
     )(*[pltpu.with_memory_space_constraint(r, pltpu.VMEM) for r in results])
 

time: 20.5 us -> 20.4 us (level)
  no operation moved by 1% of the time
where the time goes in v4:
time: 20.4 us; the launch traced here: 20.2 us
  Pallas kernels  19.6 us (96%)
  between operations  0.64 us (3%)
    pallas_call x1, Pallas kernels, per_device(): pl.pallas_call(kernel, out_shape=tuple((vmem(*shape) for shape in kept)),...  18.2 us
    pallas_call x1, Pallas kernels, per_device(): pl.pallas_call(last_primal, out_shape=tuple((jax.ShapeDtypeStruct(shape,...  1.36 us

profile of v4, /device:TPU:0, one launch (start us, length us, event | category | flops | bytes accessed | tf_op | source)
XLA Modules:
  0.0 20.2 jit_solution(328870522236148902)
XLA Ops:
  0.6 18.2 %tgv.1 = (f32[8,32,128]{2,1,0:T(8,128)S(1)}, f32[3,8,32,128]{3,2,1,0:T(8,128)S(1)}, f32[3,8,32,128]{3,2,1,0:T(8,128)S(1)}, f32[6,8,32,128]{3,2,1,0:T(8,128)S(1)}...) custom-call(f32[8,32,128]{2,1,0:T(8,128)} %noisy_in.1, ...), custom_call_target="tpu_custom_call" | custom-call | tf_op jit(solution)/shard_map/tgv/pallas_call | solution.py:763
  18.9 1.4 %out.1 = (f32[8,32,128]{2,1,0:T(8,128)}, f32[3,8,32,128]{3,2,1,0:T(8,128)}, f32[3,8,32,128]{3,2,1,0:T(8,128)}, f32[6,8,32,128]{3,2,1,0:T(8,128)}) custom-call(f32[8,32,128]{2,1,0:T(8,128)S(1)} %get-tuple-element.13.u_in, f32[3,8,32,128]{3,2,1,0:T(8,128)S(1)} %get-tuple-element.14.v_in, f32[3,8,32,128]{3,2,1,0:T(8,128)S(1)} %get-tuple-element.15.p_in, ...), custom_call_target="tpu_custom_call" | custom-call | tf_op jit(solution)/shard_map/out/pallas_call | solution.py:803

commit v5 on v4

--- a/solution.py
+++ b/solution.py
@@ -70,7 +70,7 @@
     u_out, v_out, p_out, q_out, gain, offset, cp, edge_y, edge_z,
     bar, face,
     z_lo, z_hi, x_lo, x_hi, y_lo, y_hi, d_a, d_b, d_c, d_d, d_e, d_g,
-    zp, zq, yp, yq, xs_own, xp, xq, cv, xe, part_p, part_q,
+    zp, zq, yp, yq, xs_own, xp, xq, cv, xe, part_p, part_q, tz_p, tz_q,
     load_sem, send_sem, recv_sem, first_send, first_recv,
 ):
     zs, ys, xs = u_in.shape
@@ -81,6 +81,7 @@
     count = [lax.axis_size(a) for a in AXES]
     below = [place[i] > 0 for i in range(3)]
     above = [place[i] < count[i] - 1 for i in range(3)]
+
 
     def exists(way):
         there = None
@@ -272,8 +273,8 @@
     duals = [
         (message(src, dst, way, first_send.at[k], first_recv.at[k]), goes[way], comes[way])
         for k, (src, dst, way) in enumerate((
-            (p_out.at[:, zs - 1], zp, Z_UP),
-            (q_out.at[:, 0], zq, Z_DOWN),
+            (tz_p, zp, Z_UP),
+            (tz_q, zq, Z_DOWN),
             (p_in.at[:, :, ys - 1], yp, Y_UP),
             (q_in.at[:, :, 0], yq, Y_DOWN),
             (xs_own, xp, X_UP),
@@ -281,9 +282,9 @@
         ))
     ]
 
-    def start(moves):
+    def start(moves, only=None):
         for copy, there, _ in moves:
-            @pl.when(there)
+            @pl.when(there if only is None else jnp.logical_and(there, only))
             def _():
                 copy.start()
 
@@ -310,25 +311,39 @@
 
         return lax.fori_loop(0, (high - low) // 2, turn, tuple(carry))
 
-    def dual_inside(z, _):
-        later = []
-        z_up, z_lo_ = up_z(z), lo_z(z)
-        for b in range(blocks):
-            r = rows(b)
+    def dual_block(z, b, for_p=True, for_q=True):
+        r = rows(b)
+        v = [bar[1 + k, z, r, :] for k in range(3)]
+        p = q = None
+        if for_p:
             u = bar[0, z, r, :]
-            v = [bar[1 + k, z, r, :] for k in range(3)]
             slopes = (
                 next_x(u) - up_x * u,
                 next_y(bar, 0, z, b, u) - up_y(b, u),
-                next_z(bar, 0, z, b) - z_up * u,
+                next_z(bar, 0, z, b) - up_z(z) * u,
             )
-            for k in range(3):
-                later.append((p_out, (k, z, r), p_out[k, z, r, :] + SIGMA * (slopes[k] - v[k])))
+            p = [p_out[k, z, r, :] + SIGMA * (slopes[k] - v[k]) for k in range(3)]
+        if for_q:
             dx = [lo_x * v[k] - prev_x(v[k]) for k in range(3)]
             dy = [lo_y(b, v[k]) - prev_y(bar, 1 + k, z, b, v[k]) for k in range(3)]
-            dz = [z_lo_ * v[k] - prev_z(bar, 1 + k, z, b) for k in range(3)]
-            for k, new in enumerate(grow_q([q_out[k, z, r, :] for k in range(6)], dx, dy, dz)):
-                later.append((q_out, (k, z, r), new))
+            dz = [lo_z(z) * v[k] - prev_z(bar, 1 + k, z, b) for k in range(3)]
+            q = grow_q([q_out[k, z, r, :] for k in range(6)], dx, dy, dz)
+        return p, q
+
+    def dual_inside(z, _):
+        later = []
+        for b in range(blocks):
+            p, q = dual_block(z, b)
+            later += [(p_out, (k, z, rows(b)), new) for k, new in enumerate(p)]
+            later += [(q_out, (k, z, rows(b)), new) for k, new in enumerate(q)]
+        flush(later)
+
+    def dual_first():
+        later = []
+        for b in range(blocks):
+            p, q = dual_block(zs - 1, b, for_q=False)[0], dual_block(0, b, for_p=False)[1]
+            later += [(tz_p, (k, rows(b)), new) for k, new in enumerate(p)]
+            later += [(tz_q, (k, rows(b)), new) for k, new in enumerate(q)]
         flush(later)
 
     def line_up(s):
@@ -599,44 +614,40 @@
         pl.semaphore_wait(barrier, peers)
     with jax.named_scope("send_z0"):
         start(exchanges[0][:2])
-        start(duals[2:4])
-        for load in loads[8:]:
-            load.start()
-    with jax.named_scope("load_face"):
         for load in loads[2:6]:
             load.wait()
         start(exchanges[0][4:6])
-    with jax.named_scope("pack_uv"):
+    with jax.named_scope("load_pq"):
+        for load in loads[6:8]:
+            load.wait()
+        for load in loads[8:]:
+            load.start()
+    with jax.named_scope("first_z"):
         packed = [empty, empty]
         for z in ends:
             pack_plane(packed, z)
+        dual_first()
         xe[0] = packed[0]
         xe[1] = packed[1]
+        start(exchanges[0][8:])
+        start(duals[:2])
+    with jax.named_scope("pack_uv"):
         for z in middle:
             pack_plane(packed, z)
         face[4] = packed[0]
         face[5] = packed[1]
-        start(exchanges[0][8:])
         start(exchanges[0][6:8])
         start(exchanges[0][2:4])
-    with jax.named_scope("load_pq"):
-        for load in loads[6:8]:
-            load.wait()
+        start(duals[2:4])
     with jax.named_scope("pack_pq"):
         packed = [empty] * 6
-        for z in ends:
-            pack_dual(packed, z)
-        for z in ends:
-            dual_inside(z, None)
-        start(duals[:2])
-    with jax.named_scope("pack_pq_rest"):
-        for z in middle:
+        for z in range(zs):
             pack_dual(packed, z)
         for k in range(6):
             xs_own[k] = packed[k]
         start(duals[4:])
     with jax.named_scope("inside0"):
-        each(1, zs - 1, dual_inside, ())
+        each(0, zs, dual_inside, ())
     with jax.named_scope("prepare"):
         for load in loads[8:]:
             load.wait()
@@ -791,6 +802,8 @@
             vmem(2, 8, xs),
             vmem(3, ys, xs),
             vmem(6, ys, xs),
+            vmem(3, ys, xs),
+            vmem(6, ys, xs),
             pltpu.SemaphoreType.DMA((12,)),
             pltpu.SemaphoreType.DMA((ITERS, 12)),
             pltpu.SemaphoreType.DMA((ITERS, 12)),

time: 20.4 us -> 20.1 us (0.985)
  Pallas kernels: 19.6 us -> 19.3 us
    pallas_call x1, Pallas kernels: 18.2 us -> 18 us  [per_device(): pl.pallas_call(kernel, out_shape=tuple((vmem(*shape) for shape in kept)),...]
where the time goes in v5:
time: 20.1 us; the launch traced here: 20 us
  Pallas kernels  19.3 us (96%)
  between operations  0.64 us (3%)
    pallas_call x1, Pallas kernels, per_device(): pl.pallas_call(kernel, out_shape=tuple((vmem(*shape) for shape in kept)),...  18 us
    pallas_call x1, Pallas kernels, per_device(): pl.pallas_call(last_primal, out_shape=tuple((jax.ShapeDtypeStruct(shape,...  1.36 us

profile of v5, /device:TPU:0, one launch (start us, length us, event | category | flops | bytes accessed | tf_op | source)
XLA Modules:
  0.0 20.0 jit_solution(12234113488400357641)
XLA Ops:
  0.6 18.0 %tgv.1 = (f32[8,32,128]{2,1,0:T(8,128)S(1)}, f32[3,8,32,128]{3,2,1,0:T(8,128)S(1)}, f32[3,8,32,128]{3,2,1,0:T(8,128)S(1)}, f32[6,8,32,128]{3,2,1,0:T(8,128)S(1)}...) custom-call(f32[8,32,128]{2,1,0:T(8,128)} %noisy_in.1, ...), custom_call_target="tpu_custom_call" | custom-call | tf_op jit(solution)/shard_map/tgv/pallas_call | solution.py:774
  18.6 1.4 %out.1 = (f32[8,32,128]{2,1,0:T(8,128)}, f32[3,8,32,128]{3,2,1,0:T(8,128)}, f32[3,8,32,128]{3,2,1,0:T(8,128)}, f32[6,8,32,128]{3,2,1,0:T(8,128)}) custom-call(f32[8,32,128]{2,1,0:T(8,128)S(1)} %get-tuple-element.13.u_in, f32[3,8,32,128]{3,2,1,0:T(8,128)S(1)} %get-tuple-element.14.v_in, f32[3,8,32,128]{3,2,1,0:T(8,128)S(1)} %get-tuple-element.15.p_in, ...), custom_call_target="tpu_custom_call" | custom-call | tf_op jit(solution)/shard_map/out/pallas_call | solution.py:816

commit v6 on v5

--- a/solution.py
+++ b/solution.py
@@ -19,7 +19,7 @@
 )
 
 
-def primal_plane(z, below, above, u_ref, v_ref, p_ref, q_ref, gain, offset, halo):
+def primal_plane(z, below, above, u_ref, v_ref, p_ref, q_ref, gain, offset, halo, only=None):
     zs, ys, xs = u_ref.shape
     blocks = ys // 8
     cp, row_p, row_q, plane_p, plane_q = halo
@@ -35,7 +35,7 @@
     lo_x = jnp.where(first_lane, factor(below[0]), 1.0)
     up_z = factor(above[2]) if z == zs - 1 else 1.0
     lo_z = factor(below[2]) if z == 0 else 1.0
-    for b in range(blocks):
+    for b in range(blocks) if only is None else only:
         r = pl.ds(8 * b, 8)
         up_y = jnp.where(last_row, factor(above[1]), 1.0) if b == blocks - 1 else 1.0
         lo_y = jnp.where(first_row, factor(below[1]), 1.0) if b == 0 else 1.0
@@ -248,13 +248,15 @@
             device_id=target(WAYS[way]), device_id_type=MESH,
         )
 
+    ahead_rows, early = ys - 8, 8 * (blocks // 2)
     exchanges = []
     for s in range(ITERS):
         z_up_part = pl.ds(1, 3) if s == 0 else pl.ds(0, 4)
         z_down_part = pl.ds(0, 1) if s == 0 else pl.ds(0, 4)
+        z_rows = pl.ds(early, ys - early) if s == 1 else pl.ds(0, ys)
         ends = (
-            (bar.at[z_up_part, zs - 1], z_lo.at[s, z_up_part]),
-            (bar.at[z_down_part, 0], z_hi.at[s, z_down_part]),
+            (bar.at[z_up_part, zs - 1, z_rows], z_lo.at[s, z_up_part, z_rows]),
+            (bar.at[z_down_part, 0, z_rows], z_hi.at[s, z_down_part, z_rows]),
             (face.at[xf], x_lo.at[s]),
             (face.at[xf], x_hi.at[s]),
             (face.at[top_face], y_lo.at[s]),
@@ -273,12 +275,16 @@
     duals = [
         (message(src, dst, way, first_send.at[k], first_recv.at[k]), goes[way], comes[way])
         for k, (src, dst, way) in enumerate((
-            (tz_p, zp, Z_UP),
-            (tz_q, zq, Z_DOWN),
+            (tz_p.at[:, pl.ds(0, ahead_rows)], zp.at[:, pl.ds(0, ahead_rows)], Z_UP),
+            (tz_q.at[:, pl.ds(0, ahead_rows)], zq.at[:, pl.ds(0, ahead_rows)], Z_DOWN),
             (p_in.at[:, :, ys - 1], yp, Y_UP),
             (q_in.at[:, :, 0], yq, Y_DOWN),
             (xs_own, xp, X_UP),
             (xs_own, xq, X_DOWN),
+            (tz_p.at[:, pl.ds(ahead_rows, 8)], zp.at[:, pl.ds(ahead_rows, 8)], Z_UP),
+            (tz_q.at[:, pl.ds(ahead_rows, 8)], zq.at[:, pl.ds(ahead_rows, 8)], Z_DOWN),
+            (bar.at[:, zs - 1, pl.ds(0, early)], z_lo.at[1, :, pl.ds(0, early)], Z_UP),
+            (bar.at[:, 0, pl.ds(0, early)], z_hi.at[1, :, pl.ds(0, early)], Z_DOWN),
         ))
     ]
 
@@ -394,9 +400,9 @@
                 later.append((part_q, (k, r), q[k]) if z == 0 else (q_out, (k, z, r), q[k]))
         flush(later)
 
-    def dual_ends(s):
+    def dual_ends(s, only=range(blocks)):
         later = []
-        for b in range(blocks):
+        for b in only:
             r = rows(b)
             t = [part_p[k, r, :] for k in range(3)]
             t[2] = t[2] + SIGMA * z_hi[s, 0, r, :]
@@ -506,9 +512,9 @@
         for k in range(6):
             yq[k] = keep(above[1], q[k])
 
-    def halo_z_first():
+    def halo_z_first(only):
         later = []
-        for b in range(blocks):
+        for b in only:
             r = rows(b)
             t = [zp[k, r, :] for k in range(3)]
             edge_x = turn_lanes(d_d[0, 0], xs - 2 - 2 * (blocks * (zs - 1) + b))
@@ -578,9 +584,9 @@
         lambda k, r: zq[k, r, :],
     )
 
-    def primal(z):
+    def primal(z, only=None):
         later = []
-        for b, r, pieces in primal_plane(z, below, above, u_out, v_out, p_out, q_out, gain, offset, halo):
+        for b, r, pieces in primal_plane(z, below, above, u_out, v_out, p_out, q_out, gain, offset, halo, only):
             for k, (new, old) in enumerate(pieces):
                 later.append((u_out, (z, r), new) if k == 0 else (v_out, (k - 1, z, r), new))
                 ahead = 2.0 * new - old
@@ -631,6 +637,7 @@
         xe[1] = packed[1]
         start(exchanges[0][8:])
         start(duals[:2])
+        start(duals[6:8])
     with jax.named_scope("pack_uv"):
         for z in middle:
             pack_plane(packed, z)
@@ -645,7 +652,7 @@
             pack_dual(packed, z)
         for k in range(6):
             xs_own[k] = packed[k]
-        start(duals[4:])
+        start(duals[4:6])
     with jax.named_scope("inside0"):
         each(0, zs, dual_inside, ())
     with jax.named_scope("prepare"):
@@ -670,7 +677,7 @@
                 halo_y_inside(s)
         if s == 0:
             with jax.named_scope(f"wait_pq{s}"):
-                got(duals[2:])
+                got(duals[2:6])
                 halo_x_inside(s)
                 halo_y_inside(s)
         with jax.named_scope(f"wait_diag{s}"):
@@ -684,24 +691,42 @@
         if s == 0:
             with jax.named_scope(f"wait_zpq{s}"):
                 got(duals[:2])
-                sent(duals)
+            with jax.named_scope("early"):
+                halo_z_first(range(blocks - 1))
+                dual_ends(s, range(blocks - 1))
+                for z in ends:
+                    primal(z, range(blocks // 2))
+                start(duals[8:])
+            with jax.named_scope("middle"):
+                for z in middle:
+                    primal(z)
+            with jax.named_scope("wait_zpq_rest"):
+                got(duals[6:8])
+                sent(duals[:8])
+        elif s == 1:
+            with jax.named_scope("wait_early"):
+                got(duals[8:])
+                sent(duals[8:])
         with jax.named_scope(f"ends{s}"):
+            packed = [empty, empty]
             if s == 0:
-                halo_z_first()
+                halo_z_first([blocks - 1])
+                dual_ends(s, [blocks - 1])
+                for z in ends:
+                    primal(z, range(blocks // 2, blocks))
             else:
                 halo_z(s)
-            dual_ends(s)
-            if last:
-                edge_y[0] = yp[1]
-                edge_z[0] = zp[2]
-                for at, k in enumerate(Y_PARTS):
-                    edge_y[1 + at] = yq[k]
-                for at, k in enumerate(Z_PARTS):
-                    edge_z[1 + at] = zq[k]
-                continue
-            packed = [empty, empty]
-            for z in ends:
-                primal(z)
+                dual_ends(s)
+                if last:
+                    edge_y[0] = yp[1]
+                    edge_z[0] = zp[2]
+                    for at, k in enumerate(Y_PARTS):
+                        edge_y[1 + at] = yq[k]
+                    for at, k in enumerate(Z_PARTS):
+                        edge_z[1 + at] = zq[k]
+                    continue
+                for z in ends:
+                    primal(z)
             for z in ends:
                 pack_plane(packed, z)
             xe[0] = packed[0]
@@ -710,8 +735,9 @@
             start(exchanges[s + 1][8:])
             start(exchanges[s + 1][:2])
         with jax.named_scope(f"primal_mid{s}"):
-            for z in middle:
-                primal(z)
+            if s > 0:
+                for z in middle:
+                    primal(z)
             for z in middle:
                 pack_plane(packed, z)
             face[4] = packed[0]
@@ -807,8 +833,8 @@
             pltpu.SemaphoreType.DMA((12,)),
             pltpu.SemaphoreType.DMA((ITERS, 12)),
             pltpu.SemaphoreType.DMA((ITERS, 12)),
-            pltpu.SemaphoreType.DMA((6,)),
-            pltpu.SemaphoreType.DMA((6,)),
+            pltpu.SemaphoreType.DMA((10,)),
+            pltpu.SemaphoreType.DMA((10,)),
         ],
         compiler_params=pltpu.CompilerParams(collective_id=0, has_side_effects=True),
         name="tgv",

time: 20.1 us -> 20.1 us (level)
  no operation moved by 1% of the time
where the time goes in v6:
time: 20.1 us; the launch traced here: 20 us
  Pallas kernels  19.3 us (96%)
  between operations  0.64 us (3%)
    pallas_call x1, Pallas kernels, per_device(): pl.pallas_call(kernel, out_shape=tuple((vmem(*shape) for shape in kept)),...  18 us
    pallas_call x1, Pallas kernels, per_device(): pl.pallas_call(last_primal, out_shape=tuple((jax.ShapeDtypeStruct(shape,...  1.36 us

profile of v6, /device:TPU:0, one launch (start us, length us, event | category | flops | bytes accessed | tf_op | source)
XLA Modules:
  0.0 20.0 jit_solution(1248386502368775010)
XLA Ops:
  0.6 18.0 %tgv.1 = (f32[8,32,128]{2,1,0:T(8,128)S(1)}, f32[3,8,32,128]{3,2,1,0:T(8,128)S(1)}, f32[3,8,32,128]{3,2,1,0:T(8,128)S(1)}, f32[6,8,32,128]{3,2,1,0:T(8,128)S(1)}...) custom-call(f32[8,32,128]{2,1,0:T(8,128)} %noisy_in.1, ...), custom_call_target="tpu_custom_call" | custom-call | tf_op jit(solution)/shard_map/tgv/pallas_call | solution.py:800
  18.6 1.4 %out.1 = (f32[8,32,128]{2,1,0:T(8,128)}, f32[3,8,32,128]{3,2,1,0:T(8,128)}, f32[3,8,32,128]{3,2,1,0:T(8,128)}, f32[6,8,32,128]{3,2,1,0:T(8,128)}) custom-call(f32[8,32,128]{2,1,0:T(8,128)S(1)} %get-tuple-element.13.u_in, f32[3,8,32,128]{3,2,1,0:T(8,128)S(1)} %get-tuple-element.14.v_in, f32[3,8,32,128]{3,2,1,0:T(8,128)S(1)} %get-tuple-element.15.p_in, ...), custom_call_target="tpu_custom_call" | custom-call | tf_op jit(solution)/shard_map/out/pallas_call | solution.py:842

commit v7 on v6

--- a/solution.py
+++ b/solution.py
@@ -65,13 +65,18 @@
         yield b, r, pieces
 
 
-def kernel(
+def kernel(*refs):
+    dma = pltpu.SemaphoreType.DMA
+    pl.run_scoped(lambda *own: exchange_kernel(*own, *refs), dma((5,)), dma((12,)), dma((10,)), dma((2, 12)), dma((10,)))
+
+
+def exchange_kernel(
+    load_sem, send_sem, first_send, recv_sem, first_recv,
     noisy_in, fid_in, u_in, v_in, p_in, q_in,
     u_out, v_out, p_out, q_out, gain, offset, cp, edge_y, edge_z,
     bar, face,
     z_lo, z_hi, x_lo, x_hi, y_lo, y_hi, d_a, d_b, d_c, d_d, d_e, d_g,
     zp, zq, yp, yq, xs_own, xp, xq, cv, xe, part_p, part_q, tz_p, tz_q,
-    load_sem, send_sem, recv_sem, first_send, first_recv,
 ):
     zs, ys, xs = u_in.shape
     blocks = ys // 8
@@ -99,22 +104,32 @@
     peers = sum(there.astype(jnp.int32) for there in goes)
 
     u_face, xf, top_face = pl.ds(0, 4), pl.ds(4, 2), pl.ds(6, 4)
-    loads = [
-        pltpu.make_async_copy(u_in, bar.at[0], load_sem.at[0]),
-        pltpu.make_async_copy(v_in, bar.at[pl.ds(1, 3)], load_sem.at[1]),
-        pltpu.make_async_copy(u_in.at[:, 0], face.at[0], load_sem.at[2]),
-        pltpu.make_async_copy(v_in.at[:, :, 0], face.at[pl.ds(1, 3)], load_sem.at[3]),
-        pltpu.make_async_copy(u_in.at[:, ys - 1], face.at[6], load_sem.at[4]),
-        pltpu.make_async_copy(v_in.at[:, :, ys - 1], face.at[pl.ds(7, 3)], load_sem.at[5]),
-        pltpu.make_async_copy(q_in, q_out, load_sem.at[6]),
-        pltpu.make_async_copy(p_in, p_out, load_sem.at[7]),
-        pltpu.make_async_copy(noisy_in, offset, load_sem.at[8]),
-        pltpu.make_async_copy(fid_in, gain, load_sem.at[9]),
-        pltpu.make_async_copy(u_in, u_out, load_sem.at[10]),
-        pltpu.make_async_copy(v_in, v_out, load_sem.at[11]),
-    ]
-    for load in loads[:2]:
-        load.start()
+    def load(group, *pairs):
+        return [pltpu.make_async_copy(src, dst, load_sem.at[group]) for src, dst in pairs]
+
+    loads = (
+        load(0, (u_in, bar.at[0]), (v_in, bar.at[pl.ds(1, 3)])),
+        load(
+            1,
+            (u_in.at[:, 0], face.at[0]), (v_in.at[:, :, 0], face.at[pl.ds(1, 3)]),
+            (u_in.at[:, ys - 1], face.at[6]), (v_in.at[:, :, ys - 1], face.at[pl.ds(7, 3)]),
+        ),
+        load(2, (q_in, q_out)),
+        load(3, (p_in, p_out)),
+        load(4, (noisy_in, offset), (fid_in, gain), (u_in, u_out), (v_in, v_out)),
+    )
+    whole = (bar, face.at[pl.ds(0, 8)], q_out, p_out, q_out)
+
+    def begin(*groups):
+        for k in groups:
+            for copy in loads[k]:
+                copy.start()
+
+    def loaded(*groups):
+        for k in groups:
+            pltpu.make_async_copy(whole[k], whole[k], load_sem.at[k]).wait()
+
+    begin(0)
 
     barrier = pltpu.get_barrier_semaphore()
     for way, there in zip(WAYS, goes):
@@ -122,8 +137,7 @@
         def _():
             pl.semaphore_signal(barrier, inc=1, device_id=target(way), device_id_type=MESH)
 
-    for load in loads[2:8]:
-        load.start()
+    begin(1, 2, 3)
 
     def clear(there, *refs):
         @pl.when(jnp.logical_not(there))
@@ -269,7 +283,7 @@
             (face.at[u_face, pl.ds(zs - 1, 1)], d_g.at[s, :, pl.ds(zs - 1, 1)]),
         )
         exchanges.append([
-            (message(src, dst, k, send_sem.at[s, k], recv_sem.at[s, k]), goes[k], comes[k])
+            (message(src, dst, k, send_sem.at[k], recv_sem.at[s % 2, k]), goes[k], comes[k])
             for k, (src, dst) in enumerate(ends)
         ])
     duals = [
@@ -614,20 +628,16 @@
 
     ends, middle = (0, zs - 1), range(1, zs - 1)
     with jax.named_scope("load_uv"):
-        for load in loads[:2]:
-            load.wait()
+        loaded(0)
     with jax.named_scope("barrier"):
         pl.semaphore_wait(barrier, peers)
     with jax.named_scope("send_z0"):
         start(exchanges[0][:2])
-        for load in loads[2:6]:
-            load.wait()
+        loaded(1)
         start(exchanges[0][4:6])
     with jax.named_scope("load_pq"):
-        for load in loads[6:8]:
-            load.wait()
-        for load in loads[8:]:
-            load.start()
+        loaded(2, 3)
+        begin(4)
     with jax.named_scope("first_z"):
         packed = [empty, empty]
         for z in ends:
@@ -656,8 +666,7 @@
     with jax.named_scope("inside0"):
         each(0, zs, dual_inside, ())
     with jax.named_scope("prepare"):
-        for load in loads[8:]:
-            load.wait()
+        loaded(4)
         lax.fori_loop(0, zs, prepare, 0)
 
     for s in range(ITERS):
@@ -747,20 +756,24 @@
             start(exchanges[s + 1][2:6])
 
 
-def last_primal(
-    u_in, v_in, p_in, q_in, gain, offset, cp, edge_y, edge_z,
+def last_primal(*refs):
+    pl.run_scoped(lambda sems: finish_kernel(sems, *refs), pltpu.SemaphoreType.DMA((4,)))
+
+
+def finish_kernel(
+    sems, u_in, v_in, p_in, q_in, gain, offset, cp, edge_y, edge_z,
     u_out, v_out, p_out, q_out,
-    u_new, v_new, sems,
+    u_new, v_new,
 ):
     zs, ys, xs = u_in.shape
     place = [lax.axis_index(a) for a in AXES]
     count = [lax.axis_size(a) for a in AXES]
     below = [place[i] > 0 for i in range(3)]
     above = [place[i] < count[i] - 1 for i in range(3)]
-    copies = [pltpu.make_async_copy(q_in.at[k], q_out.at[k], sems.at[k]) for k in range(6)]
-    copies += [pltpu.make_async_copy(p_in.at[k], p_out.at[k], sems.at[6 + k]) for k in range(3)]
-    for copy in copies:
-        copy.start()
+    for k in range(6):
+        pltpu.make_async_copy(q_in.at[k], q_out.at[k], sems.at[0]).start()
+    for k in range(3):
+        pltpu.make_async_copy(p_in.at[k], p_out.at[k], sems.at[1]).start()
     halo = (
         cp,
         lambda z: edge_y[0, pl.ds(z, 1), :],
@@ -775,15 +788,10 @@
                 v_new[k, z, r, :] = pieces[1 + k][0]
         if z % 2 == 1:
             two = pl.ds(z - 1, 2)
-            mine = [
-                pltpu.make_async_copy(v_new.at[:, two], v_out.at[:, two], sems.at[9 + z - 1]),
-                pltpu.make_async_copy(u_new.at[two], u_out.at[two], sems.at[9 + z]),
-            ]
-            for copy in mine:
-                copy.start()
-            copies += mine
-    for copy in copies:
-        copy.wait()
+            pltpu.make_async_copy(v_new.at[:, two], v_out.at[:, two], sems.at[2]).start()
+            pltpu.make_async_copy(u_new.at[two], u_out.at[two], sems.at[3]).start()
+    for k, (src, dst) in enumerate(((q_in, q_out), (p_in, p_out), (v_new, v_out), (u_new, u_out))):
+        pltpu.make_async_copy(src, dst, sems.at[k]).wait()
 
 
 def per_device(noisy_image, fidelity, primal_u, primal_v, dual_p, dual_q):
@@ -830,11 +838,6 @@
             vmem(6, ys, xs),
             vmem(3, ys, xs),
             vmem(6, ys, xs),
-            pltpu.SemaphoreType.DMA((12,)),
-            pltpu.SemaphoreType.DMA((ITERS, 12)),
-            pltpu.SemaphoreType.DMA((ITERS, 12)),
-            pltpu.SemaphoreType.DMA((10,)),
-            pltpu.SemaphoreType.DMA((10,)),
         ],
         compiler_params=pltpu.CompilerParams(collective_id=0, has_side_effects=True),
         name="tgv",
@@ -847,7 +850,6 @@
         scratch_shapes=[
             vmem(zs, ys, xs),
             vmem(3, zs, ys, xs),
-            pltpu.SemaphoreType.DMA((9 + zs,)),
         ],
         name="out",
     )(*[pltpu.with_memory_space_constraint(r, pltpu.VMEM) for r in results])

time: 20.1 us -> 19 us (0.945)
  Pallas kernels: 19.3 us -> 18.2 us
    pallas_call x1, Pallas kernels: 18 us -> 17 us  [per_device(): pl.pallas_call(kernel, out_shape=tuple((vmem(*shape) for shape in kept)),...]
where the time goes in v7:
time: 19 us; the launch traced here: 18.9 us
  Pallas kernels  18.2 us (96%)
  between operations  0.64 us (3%)
    pallas_call x1, Pallas kernels, per_device(): pl.pallas_call(kernel, out_shape=tuple((vmem(*shape) for shape in kept)),...  17 us
    pallas_call x1, Pallas kernels, per_device(): pl.pallas_call(last_primal, out_shape=tuple((jax.ShapeDtypeStruct(shape,...  1.21 us

profile of v7, /device:TPU:0, one launch (start us, length us, event | category | flops | bytes accessed | tf_op | source)
XLA Modules:
  0.0 18.9 jit_solution(12550468399729672822)
XLA Ops:
  0.6 17.0 %tgv.1 = (f32[8,32,128]{2,1,0:T(8,128)S(1)}, f32[3,8,32,128]{3,2,1,0:T(8,128)S(1)}, f32[3,8,32,128]{3,2,1,0:T(8,128)S(1)}, f32[6,8,32,128]{3,2,1,0:T(8,128)S(1)}...) custom-call(f32[8,32,128]{2,1,0:T(8,128)} %refs_0_.1, ...), custom_call_target="tpu_custom_call" | custom-call | tf_op jit(solution)/shard_map/tgv/pallas_call | solution.py:808
  17.7 1.2 %out.1 = (f32[8,32,128]{2,1,0:T(8,128)}, f32[3,8,32,128]{3,2,1,0:T(8,128)}, f32[3,8,32,128]{3,2,1,0:T(8,128)}, f32[6,8,32,128]{3,2,1,0:T(8,128)}) custom-call(f32[8,32,128]{2,1,0:T(8,128)S(1)} %get-tuple-element.13.refs_0_, f32[3,8,32,128]{3,2,1,0:T(8,128)S(1)} %get-tuple-element.14.refs_1_, f32[3,8,32,128]{3,2,1,0:T(8,128)S(1)} %get-tuple-element.15.refs_2_, ...), custom_call_target="tpu_custom_call" | custom-call | tf_op jit(solution)/shard_map/out/pallas_call | solution.py:845

commit v8 on v7

--- a/solution.py
+++ b/solution.py
@@ -67,7 +67,7 @@
 
 def kernel(*refs):
     dma = pltpu.SemaphoreType.DMA
-    pl.run_scoped(lambda *own: exchange_kernel(*own, *refs), dma((5,)), dma((12,)), dma((10,)), dma((2, 12)), dma((10,)))
+    pl.run_scoped(lambda *own: exchange_kernel(*own, *refs), dma((8,)), dma((12,)), dma((10,)), dma((2, 12)), dma((10,)))
 
 
 def exchange_kernel(
@@ -107,18 +107,28 @@
     def load(group, *pairs):
         return [pltpu.make_async_copy(src, dst, load_sem.at[group]) for src, dst in pairs]
 
+    inner = pl.ds(1, zs - 2)
     loads = (
-        load(0, (u_in, bar.at[0]), (v_in, bar.at[pl.ds(1, 3)])),
+        load(0, *[
+            pair for z in (0, zs - 1)
+            for pair in ((u_in.at[z], bar.at[0, z]), (v_in.at[:, z], bar.at[pl.ds(1, 3), z]))
+        ]),
         load(
             1,
             (u_in.at[:, 0], face.at[0]), (v_in.at[:, :, 0], face.at[pl.ds(1, 3)]),
             (u_in.at[:, ys - 1], face.at[6]), (v_in.at[:, :, ys - 1], face.at[pl.ds(7, 3)]),
         ),
-        load(2, (q_in, q_out)),
-        load(3, (p_in, p_out)),
+        load(2, (q_in.at[:, 0], q_out.at[:, 0])),
+        load(3, (p_in.at[:, zs - 1], p_out.at[:, zs - 1])),
         load(4, (noisy_in, offset), (fid_in, gain), (u_in, u_out), (v_in, v_out)),
+        load(5, (u_in.at[inner], bar.at[0, inner]), (v_in.at[:, inner], bar.at[pl.ds(1, 3), inner])),
+        load(6, (q_in.at[:, pl.ds(1, zs - 1)], q_out.at[:, pl.ds(1, zs - 1)])),
+        load(7, (p_in.at[:, pl.ds(0, zs - 1)], p_out.at[:, pl.ds(0, zs - 1)])),
     )
-    whole = (bar, face.at[pl.ds(0, 8)], q_out, p_out, q_out)
+    whole = (
+        bar.at[:, pl.ds(0, 2)], face.at[pl.ds(0, 8)], tz_q, tz_p, q_out,
+        bar.at[:, inner], q_out.at[:, pl.ds(1, zs - 1)], p_out.at[:, pl.ds(0, zs - 1)],
+    )
 
     def begin(*groups):
         for k in groups:
@@ -129,7 +139,7 @@
         for k in groups:
             pltpu.make_async_copy(whole[k], whole[k], load_sem.at[k]).wait()
 
-    begin(0)
+    begin(0, 2, 3)
 
     barrier = pltpu.get_barrier_semaphore()
     for way, there in zip(WAYS, goes):
@@ -137,7 +147,7 @@
         def _():
             pl.semaphore_signal(barrier, inc=1, device_id=target(way), device_id_type=MESH)
 
-    begin(1, 2, 3)
+    begin(1, 5, 6, 7)
 
     def clear(there, *refs):
         @pl.when(jnp.logical_not(there))
@@ -367,9 +377,9 @@
         flush(later)
 
     def line_up(s):
-        cv[0] = jnp.where(odd, turn_lanes(x_hi[s, 0], half_lanes - 2), x_lo[s, 0])
-        cv[1] = turn_lanes(x_lo[s, 1], half_lanes)
-        cv[2] = x_lo[s, 1]
+        cv[0] = SIGMA * jnp.where(odd, turn_lanes(x_hi[s, 0], half_lanes - 2), x_lo[s, 0])
+        cv[1] = half * turn_lanes(x_lo[s, 1], half_lanes)
+        cv[2] = half * x_lo[s, 1]
 
     def less_q(q, x=None, y=None, z=None):
         q = list(q)
@@ -394,7 +404,7 @@
             by = half_lanes - 2 * (z * blocks + b)
             from_x = [turn_lanes(cv[k], by) for k in range(3)]
             t = [p_out[k, z, r, :] for k in range(3)]
-            t[0] = t[0] + SIGMA * jnp.where(last_lane, from_x[0], 0.0)
+            t[0] = t[0] + jnp.where(last_lane, from_x[0], 0.0)
             if b == blocks - 1:
                 t[1] = t[1] + SIGMA * jnp.where(last_row, y_hi[s, 0, pl.ds(z, 1), :], 0.0)
             for k in range(3):
@@ -407,7 +417,9 @@
             hy = None
             if b == 0:
                 hy = [jnp.where(first_row, y_lo[s, 1 + k, pl.ds(z, 1), :], 0.0) for k in range(3)]
-            q = less_q([q_out[k, z, r, :] for k in range(6)], hx, hy)
+            q = less_q([q_out[k, z, r, :] for k in range(6)], y=hy)
+            for k, part in zip((XX, XY, XZ), hx):
+                q[k] = q[k] - part
             if z > 0:
                 q = shrink_q(q)
             for k in range(6):
@@ -627,16 +639,25 @@
         return carry
 
     ends, middle = (0, zs - 1), range(1, zs - 1)
+
+    def primal_and_pack(lag=3):
+        packed = [empty, empty]
+        for z in middle:
+            primal(z)
+            if z > lag:
+                pack_plane(packed, z - lag)
+        for z in middle[-lag:]:
+            pack_plane(packed, z)
+        return packed
+
     with jax.named_scope("load_uv"):
         loaded(0)
     with jax.named_scope("barrier"):
         pl.semaphore_wait(barrier, peers)
     with jax.named_scope("send_z0"):
         start(exchanges[0][:2])
-        loaded(1)
-        start(exchanges[0][4:6])
     with jax.named_scope("load_pq"):
-        loaded(2, 3)
+        loaded(2, 3, 1)
         begin(4)
     with jax.named_scope("first_z"):
         packed = [empty, empty]
@@ -648,7 +669,9 @@
         start(exchanges[0][8:])
         start(duals[:2])
         start(duals[6:8])
+        start(exchanges[0][4:6])
     with jax.named_scope("pack_uv"):
+        loaded(5)
         for z in middle:
             pack_plane(packed, z)
         face[4] = packed[0]
@@ -657,6 +680,7 @@
         start(exchanges[0][2:4])
         start(duals[2:4])
     with jax.named_scope("pack_pq"):
+        loaded(6, 7)
         packed = [empty] * 6
         for z in range(zs):
             pack_dual(packed, z)
@@ -707,8 +731,7 @@
                     primal(z, range(blocks // 2))
                 start(duals[8:])
             with jax.named_scope("middle"):
-                for z in middle:
-                    primal(z)
+                packed = primal_and_pack()
             with jax.named_scope("wait_zpq_rest"):
                 got(duals[6:8])
                 sent(duals[:8])
@@ -717,7 +740,7 @@
                 got(duals[8:])
                 sent(duals[8:])
         with jax.named_scope(f"ends{s}"):
-            packed = [empty, empty]
+            of_ends = [empty, empty]
             if s == 0:
                 halo_z_first([blocks - 1])
                 dual_ends(s, [blocks - 1])
@@ -737,23 +760,26 @@
                 for z in ends:
                     primal(z)
             for z in ends:
-                pack_plane(packed, z)
-            xe[0] = packed[0]
-            xe[1] = packed[1]
+                pack_plane(of_ends, z)
+            xe[0] = of_ends[0]
+            xe[1] = of_ends[1]
+            if s == 0:
+                face[4] = packed[0] + of_ends[0]
+                face[5] = packed[1] + of_ends[1]
         with jax.named_scope(f"send_z{s}"):
             start(exchanges[s + 1][8:])
+            if s == 0:
+                start(exchanges[s + 1][4:8])
+                start(exchanges[s + 1][2:4])
             start(exchanges[s + 1][:2])
-        with jax.named_scope(f"primal_mid{s}"):
-            if s > 0:
-                for z in middle:
-                    primal(z)
-            for z in middle:
-                pack_plane(packed, z)
-            face[4] = packed[0]
-            face[5] = packed[1]
-        with jax.named_scope(f"send{s}"):
-            start(exchanges[s + 1][6:8])
-            start(exchanges[s + 1][2:6])
+        if s > 0:
+            with jax.named_scope(f"primal_mid{s}"):
+                packed = primal_and_pack()
+                face[4] = packed[0] + of_ends[0]
+                face[5] = packed[1] + of_ends[1]
+            with jax.named_scope(f"send{s}"):
+                start(exchanges[s + 1][4:8])
+                start(exchanges[s + 1][2:4])
 
 
 def last_primal(*refs):

time: 19 us -> 19 us (level)
  no operation moved by 1% of the time
where the time goes in v8:
time: 19 us; the launch traced here: 18.8 us
  Pallas kernels  18.2 us (96%)
  between operations  0.64 us (3%)
    pallas_call x1, Pallas kernels, per_device(): pl.pallas_call(kernel, out_shape=tuple((vmem(*shape) for shape in kept)),...  17 us
    pallas_call x1, Pallas kernels, per_device(): pl.pallas_call(last_primal, out_shape=tuple((jax.ShapeDtypeStruct(shape,...  1.21 us

profile of v8, /device:TPU:0, one launch (start us, length us, event | category | flops | bytes accessed | tf_op | source)
XLA Modules:
  0.0 18.8 jit_solution(10130980302603791399)
XLA Ops:
  0.6 17.0 %tgv.1 = (f32[8,32,128]{2,1,0:T(8,128)S(1)}, f32[3,8,32,128]{3,2,1,0:T(8,128)S(1)}, f32[3,8,32,128]{3,2,1,0:T(8,128)S(1)}, f32[6,8,32,128]{3,2,1,0:T(8,128)S(1)}...) custom-call(f32[8,32,128]{2,1,0:T(8,128)} %refs_0_.1, ...), custom_call_target="tpu_custom_call" | custom-call | tf_op jit(solution)/shard_map/tgv/pallas_call | solution.py:834
  17.6 1.2 %out.1 = (f32[8,32,128]{2,1,0:T(8,128)}, f32[3,8,32,128]{3,2,1,0:T(8,128)}, f32[3,8,32,128]{3,2,1,0:T(8,128)}, f32[6,8,32,128]{3,2,1,0:T(8,128)}) custom-call(f32[8,32,128]{2,1,0:T(8,128)S(1)} %get-tuple-element.13.refs_0_, f32[3,8,32,128]{3,2,1,0:T(8,128)S(1)} %get-tuple-element.14.refs_1_, f32[3,8,32,128]{3,2,1,0:T(8,128)S(1)} %get-tuple-element.15.refs_2_, ...), custom_call_target="tpu_custom_call" | custom-call | tf_op jit(solution)/shard_map/out/pallas_call | solution.py:871

commit v9 on v8

--- a/solution.py
+++ b/solution.py
@@ -652,13 +652,8 @@
 
     with jax.named_scope("load_uv"):
         loaded(0)
-    with jax.named_scope("barrier"):
-        pl.semaphore_wait(barrier, peers)
-    with jax.named_scope("send_z0"):
-        start(exchanges[0][:2])
     with jax.named_scope("load_pq"):
         loaded(2, 3, 1)
-        begin(4)
     with jax.named_scope("first_z"):
         packed = [empty, empty]
         for z in ends:
@@ -666,10 +661,15 @@
         dual_first()
         xe[0] = packed[0]
         xe[1] = packed[1]
+    with jax.named_scope("barrier"):
+        pl.semaphore_wait(barrier, peers)
+    with jax.named_scope("send_z0"):
         start(exchanges[0][8:])
+        start(exchanges[0][:2])
         start(duals[:2])
         start(duals[6:8])
         start(exchanges[0][4:6])
+        begin(4)
     with jax.named_scope("pack_uv"):
         loaded(5)
         for z in middle:

time: 19 us -> 19 us (level)
  no operation moved by 1% of the time
where the time goes in v9:
time: 19 us; the launch traced here: 18.8 us
  Pallas kernels  18.2 us (96%)
  between operations  0.64 us (3%)
    pallas_call x1, Pallas kernels, per_device(): pl.pallas_call(kernel, out_shape=tuple((vmem(*shape) for shape in kept)),...  17 us
    pallas_call x1, Pallas kernels, per_device(): pl.pallas_call(last_primal, out_shape=tuple((jax.ShapeDtypeStruct(shape,...  1.21 us

profile of v9, /device:TPU:0, one launch (start us, length us, event | category | flops | bytes accessed | tf_op | source)
XLA Modules:
  0.0 18.8 jit_solution(14988812986961894633)
XLA Ops:
  0.6 17.0 %tgv.1 = (f32[8,32,128]{2,1,0:T(8,128)S(1)}, f32[3,8,32,128]{3,2,1,0:T(8,128)S(1)}, f32[3,8,32,128]{3,2,1,0:T(8,128)S(1)}, f32[6,8,32,128]{3,2,1,0:T(8,128)S(1)}...) custom-call(f32[8,32,128]{2,1,0:T(8,128)} %refs_0_.1, ...), custom_call_target="tpu_custom_call" | custom-call | tf_op jit(solution)/shard_map/tgv/pallas_call | solution.py:834
  17.6 1.2 %out.1 = (f32[8,32,128]{2,1,0:T(8,128)}, f32[3,8,32,128]{3,2,1,0:T(8,128)}, f32[3,8,32,128]{3,2,1,0:T(8,128)}, f32[6,8,32,128]{3,2,1,0:T(8,128)}) custom-call(f32[8,32,128]{2,1,0:T(8,128)S(1)} %get-tuple-element.13.refs_0_, f32[3,8,32,128]{3,2,1,0:T(8,128)S(1)} %get-tuple-element.14.refs_1_, f32[3,8,32,128]{3,2,1,0:T(8,128)S(1)} %get-tuple-element.15.refs_2_, ...), custom_call_target="tpu_custom_call" | custom-call | tf_op jit(solution)/shard_map/out/pallas_call | solution.py:871
